TPU v7x, 128 devices: a whole 4x4x4 slice. The times are simulated.
128 devices in a mesh: dp: 8 (over y, core), seq: 16 (over x, z).
Axes of the slice: x: 4, y: 4, z: 4, core: 2. Of those that a mesh axis runs over, the one named last changes fastest.
Arguments:
- head_inputs: bfloat16 [8, 6144, 1024], P('dp', 'seq'), may hold values from -6 to 6
- gate_inputs: bfloat16 [8, 6144, 1024], P('dp', 'seq'), may hold values from -6 to 6
- state_proj: bfloat16 [8, 6144, 256], P('dp', 'seq'), may hold values from -2 to 2
- time_steps: float32 [8, 6144, 16], P('dp', 'seq'), may hold values from -4.7 to 4.7
- token_ids: int32 [8, 6144], P('dp', 'seq'), may hold values from 0 to 50279, as said below
- token_counts: int32 [8], replicated, may hold values from 3072 to 6144
- teacher_out: bfloat16 [8, 6144, 1024], P('dp', 'seq'), may hold values from -6 to 6
- out_weight: float32 [1024, 1024], P(('dp', 'seq')), may hold values from -0.1875 to 0.1875
- decay_log: float32 [16], replicated, may hold values from -6.5 to 1
- step_bias: float32 [16], replicated, may hold values from -5 to -3
- skip_gain: float32 [16], replicated, may hold values from 0.5 to 1.5
- norm_gain: float32 [1024], replicated, may hold values from 0.5 to 1.5
Outputs:
- losses: float32 [2], replicated
- new_weight: float32 [1024, 1024], P(('dp', 'seq'))
- new_decay: float32 [16], replicated
- new_bias: float32 [16], replicated
- new_skip: float32 [16], replicated
- new_gain: float32 [1024], replicated
Inputs may be any that keep to these rules, and one draw needn't show every extreme that they name: `token_ids`: in each sequence exactly one position, never the first, holds id 0.
All inputs are finite; a program needn't handle non-finite values.
Results may differ from a plain program's by a relative error of at most 0.0003.
Values may be sent and summed in bfloat16 or wider, within the bound.
A program may use at most 192 MiB of HBM per device.

v0:
```python
import jax
import jax.numpy as jnp
from jax import lax
from jax.sharding import Mesh
from jax.sharding import PartitionSpec as P

STEPS = 2
SEQ = ("seq_0", "seq_1")
DP = ("dp_0", "dp_1")
DP_SEQ = ("dp_0", "dp_1", "seq_0", "seq_1")


norm_floor = 1.0
clip_limit = 1.0
learn_rate = 8.0
highest = lax.Precision.HIGHEST
masked_low = -10000.0


def nothing_yet(array, identity):
    return jax.tree.map(
        lambda part, zero: jnp.zeros_like(part) + jnp.asarray(zero, part.dtype), array, identity
    )


def entering_2(array, axes, combine, identity):
    before = start = nothing_yet(array, identity)
    so_far = array
    for axis in reversed(axes):
        count, index = (lax.axis_size(axis), lax.axis_index(axis))
        pieces = jax.tree.map(lambda part: lax.all_gather(part, axis), so_far)
        inside, so_far = (start, start)
        for k in range(count):
            passed = k < index
            so_far = combine(so_far, jax.tree.map(lambda part: part[k], pieces))
            inside = jax.tree.map(lambda new, old: jnp.where(passed, new, old), so_far, inside)
        before = combine(inside, before)
    return before


def laid_out(tiles, dim):
    tiles = jnp.moveaxis(tiles, 0, dim)
    shape = tiles.shape
    return tiles.reshape(*shape[:dim], shape[dim] * shape[dim + 1], *shape[dim + 2 :])


def stacked_from(array, axes, sequence):
    tiles = array[None]
    for k in sequence:
        tiles = lax.all_gather(tiles, axes[k], axis=0, tiled=True)
    current = [lax.axis_size(axes[k]) for k in reversed(sequence)]
    tiles = tiles.reshape(*current, *array.shape)
    turned = sorted(range(len(sequence)), key=lambda place: sequence[len(sequence) - 1 - place])
    return tiles.transpose(*turned, *range(len(sequence), tiles.ndim)).reshape(-1, *array.shape)


def gather_axes(array, axes, sequence, dim):
    return laid_out(stacked_from(array, axes, sequence), dim)


def prefix_by_axis(array, axes, combine, identity):
    before = start = nothing_yet(array, identity)
    so_far = array
    for axis in reversed(axes):
        count, index = (lax.axis_size(axis), lax.axis_index(axis))
        pieces = jax.tree.map(
            lambda part, kind: lax.all_gather(part.astype(kind), axis),
            so_far,
            jax.tree.map(lambda a: jnp.bfloat16 if a.dtype == jnp.float32 else a.dtype, array),
        )
        inside, so_far = (start, start)
        for k in reversed(range(count)):
            passed = k > index
            so_far = combine(
                so_far, jax.tree.map(lambda part, own: part[k].astype(own.dtype), pieces, array)
            )
            inside = jax.tree.map(lambda new, old: jnp.where(passed, new, old), so_far, inside)
        before = combine(inside, before)
    return before


def split_up(array, dim, count):
    shape = array.shape
    tiles = array.reshape(*shape[:dim], count, shape[dim] // count, *shape[dim + 1 :])
    return jnp.moveaxis(tiles, dim, 0)


def sent_and_summed(array, axis, dim):
    count = lax.axis_size(axis)
    tiles = lax.all_to_all(split_up(array, dim, count), axis, 0, 0, tiled=True)
    return jnp.sum(tiles, axis=0)


def collected_together(array, axis):
    leaves = jax.tree.leaves(array)
    sequence = sorted(range(len(leaves)), key=lambda k: -leaves[k].size)
    width = (1, *leaves[sequence[0]].shape)[-1]
    lines = [
        jnp.pad(leaves[k].reshape(-1), (0, -leaves[k].size % width)).reshape(-1, width)
        for k in sequence
    ]
    both, at, found = (lax.all_gather(jnp.concatenate(lines), axis), 0, {})
    for k, line in zip(sequence, lines):
        slab = both[:, at : at + len(line)].reshape(len(both), -1)
        found[k] = slab[:, : leaves[k].size].reshape(-1, *leaves[k].shape)
        at += len(line)
    numbers = iter(range(len(leaves)))
    return jax.tree.map(lambda _: found[next(numbers)], array)


def gathered_by_type(array, axis):
    leaves, found = (jax.tree.leaves(array), {})
    for first, a in enumerate(leaves):
        if first not in found:
            alike = [k for k, b in enumerate(leaves) if b.dtype == a.dtype]
            got = (
                collected_together([leaves[k] for k in alike], axis)
                if len(alike) > 1
                else [lax.all_gather(a, axis)]
            )
            for k, b in zip(alike, got):
                found[k] = b
    numbers = iter(range(len(leaves)))
    return jax.tree.map(lambda _: found[next(numbers)], array)


def combined_by_axis(array, axes, combine):
    for axis in axes:
        pieces = gathered_by_type(array, axis)
        array = jax.tree.map(lambda part: part[0], pieces)
        for k in range(1, lax.axis_size(axis)):
            array = combine(array, jax.tree.map(lambda part: part[k], pieces))
    return array


def step_sizes(decay_log, step_bias, step_raw):
    step_width = jax.nn.softplus(step_raw + step_bias[None, :])
    decay_sum = jnp.cumsum(step_width * (-jnp.exp(decay_log))[None, :], axis=0)
    return (step_width, decay_sum)


def mix_block(
    decay_log,
    step_bias,
    skip_gain,
    norm_gain,
    state_in,
    head_inputs,
    gate_inputs,
    b_proj,
    c_proj,
    step_raw,
    segment,
):
    positions = head_inputs.shape[0]
    head_count = decay_log.shape[0]
    step_width, decay_sum = step_sizes(decay_log, step_bias, step_raw)
    inputs_f = head_inputs.astype(jnp.float32).reshape(positions, head_count, -1)
    scaled = inputs_f * step_width[:, :, None]
    scores = jnp.dot(c_proj, b_proj.T, preferred_element_type=jnp.float32)
    position = jnp.arange(positions)
    allowed = (segment[:, None] == segment[None, :]) & (position[:, None] >= position[None, :])

    def one_head(head_data):
        head_sum, head_scaled = head_data
        spread = head_sum[:, None] - head_sum[None, :]
        decay_grid = jnp.exp(jnp.where(allowed, spread, masked_low))
        return jnp.dot(decay_grid * scores, head_scaled, precision=highest)

    intra_sum = jnp.transpose(
        lax.map(one_head, (decay_sum.T, jnp.transpose(scaled, (1, 0, 2)))), (1, 0, 2)
    )
    entry_decay = jnp.exp(decay_sum) * (segment == 0)[:, None]
    carried = (
        jnp.einsum("in,hpn->ihp", c_proj.astype(jnp.float32), state_in, precision=highest)
        * entry_decay[:, :, None]
    )
    mixed_out = intra_sum + carried + skip_gain[None, :, None] * inputs_f
    gated = mixed_out.reshape(positions, -1) * jax.nn.silu(gate_inputs.astype(jnp.float32))
    mean_square = jnp.mean(gated * gated, axis=1, keepdims=True)
    return gated * norm_gain[None, :] * lax.rsqrt(mean_square + norm_floor)


def state_block(decay_log, step_bias, head_inputs, b_proj, step_raw, segment):
    positions = head_inputs.shape[0]
    head_count = decay_log.shape[0]
    step_width, decay_sum = step_sizes(decay_log, step_bias, step_raw)
    final_sum = decay_sum[-1]
    same_doc = (segment == segment[-1])[:, None]
    tail_decay = jnp.exp(jnp.where(same_doc, final_sum[None, :] - decay_sum, masked_low))
    inputs_f = head_inputs.astype(jnp.float32).reshape(positions, head_count, -1)
    weighted = inputs_f * (step_width * tail_decay)[:, :, None]
    state_out = jnp.einsum("jhp,jn->hpn", weighted, b_proj.astype(jnp.float32), precision=highest)
    carry_out = jnp.exp(final_sum) * (segment[-1] == 0)
    return (carry_out, state_out)


def combine_states(earlier, later):
    return (earlier[0] * later[0], later[0][:, None, None] * earlier[1] + later[1])


def combine_sums(first_part, second_part):
    summed_up = first_part[5] + second_part[5]
    back_part = summed_up - first_part[5]
    lost_part = first_part[5] - (summed_up - back_part) + (second_part[5] - back_part)
    grads_part = tuple(
        (left_item + right_item for left_item, right_item in zip(first_part[:5], second_part[:5]))
    )
    return grads_part + (summed_up, first_part[6] + second_part[6] + lost_part)


def per_device(
    head_inputs,
    gate_inputs,
    state_proj,
    time_steps,
    token_ids,
    token_counts,
    teacher_out,
    out_weight,
    decay_log,
    step_bias,
    skip_gain,
    norm_gain,
):
    tok_rows = head_inputs.shape[1]
    inner_width = head_inputs.shape[2]
    state_size = state_proj.shape[2] // 2
    model_width = teacher_out.shape[2]
    head_count = decay_log.shape[0]
    head_size = inner_width // head_count
    inputs_local = head_inputs[0]
    gates_local = gate_inputs[0]
    b_proj = state_proj[0, :, :state_size]
    c_proj = state_proj[0, :, state_size:]
    raw_local = time_steps[0]
    segment = jnp.cumsum((token_ids[0] == 0).astype(jnp.int32))
    position = lax.axis_index(SEQ) * tok_rows + jnp.arange(tok_rows, dtype=jnp.int32)
    own_count = lax.dynamic_index_in_dim(token_counts, lax.axis_index(DP), keepdims=False)
    scored = (position < own_count).astype(jnp.float32)
    total_count = jnp.sum(token_counts).astype(jnp.float32)
    target_f = teacher_out[0].astype(jnp.float32)
    identity = (
        jnp.ones((head_count,), jnp.float32),
        jnp.zeros((head_count, head_size, state_size), jnp.float32),
    )
    losses = []
    for step_index in range(STEPS):
        weight_b = out_weight.astype(jnp.bfloat16)

        def state_part(decay_arg, bias_arg):
            return state_block(decay_arg, bias_arg, inputs_local, b_proj, raw_local, segment)

        (carry_out, state_out), state_pull = jax.vjp(state_part, decay_log, step_bias)
        state_in = entering_2((carry_out, state_out), SEQ, combine_states, identity)[1]

        def mix_part(decay_arg, bias_arg, skip_arg, gain_arg, entering):
            return mix_block(
                decay_arg,
                bias_arg,
                skip_arg,
                gain_arg,
                entering,
                inputs_local,
                gates_local,
                b_proj,
                c_proj,
                raw_local,
                segment,
            )

        normed, mix_pull = jax.vjp(mix_part, decay_log, step_bias, skip_gain, norm_gain, state_in)
        normed_b = normed.astype(jnp.bfloat16)
        output = jnp.dot(
            normed_b,
            gather_axes(weight_b, DP_SEQ, (0, 2, 3, 1), 0),
            preferred_element_type=jnp.float32,
        )
        residual = output - target_f
        token_loss = jnp.sum(residual * residual, axis=1) * scored / model_width
        loss_part = jnp.sum(token_loss)
        out_grad = (residual * (2.0 / (model_width * total_count)) * scored[:, None]).astype(
            jnp.bfloat16
        )
        weight_grad = jnp.dot(normed_b.T, out_grad, preferred_element_type=jnp.float32)
        normed_grad = jnp.dot(
            out_grad,
            lax.all_gather(weight_b, DP_SEQ, axis=0, tiled=True).T,
            preferred_element_type=jnp.float32,
        )
        decay_one, bias_one, skip_grad, gain_grad, state_grad = mix_pull(normed_grad)
        after_grad = prefix_by_axis((carry_out, state_grad), SEQ, combine_states, identity)[1]
        carry_grad = jnp.sum(after_grad * state_in, axis=(1, 2))
        decay_two, bias_two = state_pull((carry_grad, after_grad))
        decay_grad = decay_one + decay_two
        bias_grad = bias_one + bias_two
        grouped = weight_grad.reshape(lax.axis_size(DP), lax.axis_size(SEQ), -1, model_width)
        by_block = sent_and_summed(grouped, SEQ, 1)
        grad_rows = sent_and_summed(by_block, DP, 0).reshape(-1, model_width)
        merged = combined_by_axis(
            (
                decay_grad,
                bias_grad,
                skip_grad,
                gain_grad,
                jnp.sum(grad_rows * grad_rows),
                loss_part,
                jnp.zeros((), jnp.float32),
            ),
            DP_SEQ,
            combine_sums,
        )
        decay_grad, bias_grad, skip_grad, gain_grad = (merged[0], merged[1], merged[2], merged[3])
        norm_square = (
            merged[4]
            + jnp.sum(decay_grad * decay_grad)
            + jnp.sum(bias_grad * bias_grad)
            + jnp.sum(skip_grad * skip_grad)
            + jnp.sum(gain_grad * gain_grad)
        )
        losses.append((merged[5] + merged[6]) / total_count)
        factor = clip_limit / jnp.maximum(jnp.sqrt(norm_square), clip_limit)
        out_weight = out_weight - learn_rate * factor * grad_rows
        decay_log = decay_log - learn_rate * factor * decay_grad
        step_bias = step_bias - learn_rate * factor * bias_grad
        skip_gain = skip_gain - learn_rate * factor * skip_grad
        norm_gain = norm_gain - learn_rate * factor * gain_grad
    return (jnp.stack(losses), out_weight, decay_log, step_bias, skip_gain, norm_gain)


def solution(mesh):
    split = Mesh(mesh.devices.reshape(4, 2, 4, 4), ("dp_0", "dp_1", "seq_0", "seq_1"))
    placed = (
        P(DP, SEQ, None),
        P(DP, SEQ, None),
        P(DP, SEQ, None),
        P(DP, SEQ, None),
        P(DP, SEQ),
        P(),
        P(DP, SEQ, None),
        P(DP_SEQ, None),
        P(),
        P(),
        P(),
        P(),
    )
    return jax.shard_map(
        per_device,
        mesh=split,
        in_specs=placed,
        out_specs=(P(), P(DP_SEQ, None), P(), P(), P(), P()),
        check_vma=False,
    )
```

profile of v0, /device:TPU:1, one launch (start us, length us, event | category | flops | bytes accessed | tf_op | source)
XLA Modules:
  0.0 913.3 jit_solution(15274373993422622586)
XLA Ops:
  8.0 10.4 %all-gather.1 = bf16[32,1024]{1,0:T(8,128)(2,1)S(1)} all-gather(bf16[8,1024]{1,0:T(8,128)(2,1)S(1)} %convert_element_type.554), channel_id=3, replica_groups=mesh['dp_0'=4,'dp_1'=2,'seq_0'=4,'seq_1'=4] {'dp_0'}, dimensions={0}, use_global_device_ids=true | all-gather | bytes 81920 | tf_op jit(solution)/shard_map/all_gather | solution.py:50
  18.3 10.4 %all_gather.156 = bf16[16,8,1024]{2,1,0:T(8,128)(2,1)} all-gather(bf16[4,8,1024]{2,1,0:T(8,128)(2,1)S(1)} %bitcast.1444), channel_id=1, replica_groups=mesh['dp_0'=4,'dp_1'=2,'seq_0'=4,'seq_1'=4] {'seq_0'}, dimensions={0}, use_global_device_ids=true | all-gather | bytes 327680 | tf_op jit(solution)/shard_map/all_gather | solution.py:50
  44.1 13.9 %all-gather.47.cloned.1.call-done = bf16[64,8,1024]{2,1,0:T(8,128)(2,1)} async-done(((bf16[16,8,1024]{2,1,0:T(8,128)(2,1)}), bf16[64,8,1024]{2,1,0:T(8,128)(2,1)}) %all-gather.47.cloned.1.call-update) | async-done | bytes 1048592 | tf_op jit(solution)/shard_map/all_gather | solution.py:50
  58.1 6.9 all-gather.14
  65.5 27.3 %all-gather.65.cloned.1.call-done = f32[64,64,128]{2,1,0:T(8,128)} async-done(((f32[16,64,128]{2,1,0:T(8,128)}), f32[64,64,128]{2,1,0:T(8,128)}) %all-gather.65.cloned.1.call-update) | async-done | bytes 2097168 | tf_op jit(solution)/shard_map/all_gather | solution.py:31
  97.8 3.4 copy.180
  102.5 4.9 broadcast.684.clone
  107.4 4.6 broadcast.684.clone.1
  112.1 60.6 %while.66 = (s32[]{:T(128)}, f32[16,384,64]{1,2,0:T(8,128)}, f32[16,384,384]{2,1,0:T(8,128)}, f32[16,384,384]{2,1,0:T(8,128)}, f32[16,384]{1,0:T(8,128)S(1)}, /*...) while((s32[]{:T(128)}, f32[16,384,64]{1,2,0:T(8,128)}, ...), condition=%wide.region_5.7_spmd.clone, body=%wide.region_4.6_spmd.clone.sunk | while | flops 115015680 | bytes 2674797 | solution.py:171
  179.2 3.1 copy.191
  182.3 7.9 all-gather.15
  192.0 3.2 copy.185
  195.2 7.0 multiply_reduce_fusion.7
  202.3 3.1 copy.183
  210.4 5.0 multiply_reduce_fusion.5
  220.0 3.1 copy.192
  226.2 6.0 all-gather.16
  232.2 6.8 all-gather.17
  239.0 3.0 copy.186
  244.4 3.0 convolution_bitcast_fusion.5
  249.8 4.6 all-to-all-start
  258.2 71.2 %while.67 = (s32[]{:T(128)}, f32[16,384]{1,0:T(8,128)S(1)}, f32[16,384,64]{1,2,0:T(8,128)}, f32[16,384,64]{1,2,0:T(8,128)}, f32[16,384,64]{2,1,0:T(8,128)}, /*in...) while((s32[]{:T(128)}, f32[16,384]{1,0:T(8,128)S(1)}, ...), condition=%wide.region_14.16_spmd.clone, body=%wide.region_11.15_spmd.clone.sunk | while | flops 227672064 | bytes 2282125 | solution.py:171
  331.6 3.7 reduce-window.55
  344.4 3.7 fusion.112
  349.0 3.7 reduce-window.59
  353.5 3.2 reduce_sum.532
  356.7 9.0 all-to-all-start.1
  367.5 4.7 all-to-all-done.1
  374.3 9.1 all-gather.18
  396.4 5.4 all-gather.19
  409.4 10.0 %all-gather.20 = f32[4,7,1024]{2,1,0:T(8,128)S(1)} all-gather(f32[1,7,1024]{2,1,0:T(8,128)S(1)} %bitcast.1447), channel_id=7, replica_groups=mesh['dp_0'=4,'dp_1'=2,'seq_0'=4,'seq_1'=4] {'seq_0'}, dimensions={0}, use_global_device_ids=true | all-gather | bytes 143360 | tf_op jit(solution)/shard_map/all_gather | solution.py:102
  432.5 9.4 %all-gather.21 = f32[4,7,1024]{2,1,0:T(8,128)S(1)} all-gather(f32[1,7,1024]{2,1,0:T(8,128)S(1)} %bitcast.1448), channel_id=8, replica_groups=mesh['dp_0'=4,'dp_1'=2,'seq_0'=4,'seq_1'=4] {'seq_1'}, dimensions={0}, use_global_device_ids=true | all-gather | bytes 143360 | tf_op jit(solution)/shard_map/all_gather | solution.py:102
  451.4 9.0 all-gather.8
  460.4 10.3 %all_gather.179 = bf16[16,8,1024]{2,1,0:T(8,128)(2,1)} all-gather(bf16[4,8,1024]{2,1,0:T(8,128)(2,1)S(1)} %bitcast.1445), channel_id=1, replica_groups=mesh['dp_0'=4,'dp_1'=2,'seq_0'=4,'seq_1'=4] {'seq_0'}, dimensions={0}, use_global_device_ids=true | all-gather | bytes 327680 | tf_op jit(solution)/shard_map/all_gather | solution.py:50
  474.0 3.0 copy.204
  480.0 3.0 copy.205
  486.0 16.2 %all-gather.57.cloned.1.call-done = bf16[64,8,1024]{2,1,0:T(8,128)(2,1)} async-done(((bf16[16,8,1024]{2,1,0:T(8,128)(2,1)}), bf16[64,8,1024]{2,1,0:T(8,128)(2,1)}) %all-gather.57.cloned.1.call-update) | async-done | bytes 1048592 | tf_op jit(solution)/shard_map/all_gather | solution.py:50
  502.3 6.9 all-gather.22
  509.7 27.3 %all-gather.69.cloned.1.call-done = f32[64,64,128]{2,1,0:T(8,128)} async-done(((f32[16,64,128]{2,1,0:T(8,128)}), f32[64,64,128]{2,1,0:T(8,128)}) %all-gather.69.cloned.1.call-update) | async-done | bytes 2097168 | tf_op jit(solution)/shard_map/all_gather | solution.py:31
  541.6 3.4 copy.203
  546.2 5.0 broadcast.684
  551.2 4.6 broadcast.684.clone.2
  555.9 60.7 %while.68 = (s32[]{:T(128)}, f32[16,384,64]{1,2,0:T(8,128)}, f32[16,384,384]{2,1,0:T(8,128)}, f32[16,384,384]{2,1,0:T(8,128)}, f32[16,384]{1,0:T(8,128)S(1)}, /*...) while((s32[]{:T(128)}, f32[16,384,64]{1,2,0:T(8,128)}, ...), condition=%wide.region_41.43_spmd.clone, body=%wide.region_40.42_spmd.clone.sunk | while | flops 115015680 | bytes 2674797 | solution.py:171
  616.7 5.3 all-gather.24
  624.0 3.1 copy.213
  627.1 7.8 all-gather.23
  636.1 3.2 copy.207
  639.3 6.9 multiply_reduce_fusion.3
  646.2 3.2 copy.206
  654.4 3.2 fusion.436
  663.0 3.1 copy.214
  669.1 5.8 all-gather.25
  694.4 4.6 all-to-all-start.2
  702.8 71.1 %while.69 = (s32[]{:T(128)}, f32[16,384]{1,0:T(8,128)S(1)}, f32[16,384,64]{1,2,0:T(8,128)}, f32[16,384,64]{1,2,0:T(8,128)}, f32[16,384,64]{2,1,0:T(8,128)}, /*in...) while((s32[]{:T(128)}, f32[16,384]{1,0:T(8,128)S(1)}, ...), condition=%wide.region_49.51_spmd.clone, body=%wide.region_46.50_spmd.clone.sunk | while | flops 227672064 | bytes 2282125 | solution.py:171
  776.1 3.7 reduce-window.65
  786.9 3.4 fusion.106
  791.3 3.7 reduce-window.69
  795.2 3.2 reduce_sum.623
  798.3 10.9 %all-to-all-start.3 = ((f32[8,1,1,8,1024]{4,3,2,1,0:T(8,128)}), f32[8,1,1,8,1024]{4,3,2,1,0:T(8,128)S(1)}, u32[]{:S(2)}, u32[]{:S(2)}) async-start(f32[8,1,1,8,1024]{4,3,2,1,0:T(8,128)} %bitcast.244), calls=%async_computation.3 | async-start | bytes 524288 | tf_op jit(solution)/shard_map/all_to_all | solution.py:90
  809.6 6.1 all-to-all-done.3
  817.1 9.1 all-gather.26
  839.3 5.4 all-gather.27
  852.5 10.0 %all-gather.28 = f32[4,7,1024]{2,1,0:T(8,128)S(1)} all-gather(f32[1,7,1024]{2,1,0:T(8,128)S(1)} %bitcast.1451), channel_id=14, replica_groups=mesh['dp_0'=4,'dp_1'=2,'seq_0'=4,'seq_1'=4] {'seq_0'}, dimensions={0}, use_global_device_ids=true | all-gather | bytes 143360 | tf_op jit(solution)/shard_map/all_gather | solution.py:102
  875.6 9.5 %all-gather.29 = f32[4,7,1024]{2,1,0:T(8,128)S(1)} all-gather(f32[1,7,1024]{2,1,0:T(8,128)S(1)} %bitcast.1452), channel_id=15, replica_groups=mesh['dp_0'=4,'dp_1'=2,'seq_0'=4,'seq_1'=4] {'seq_1'}, dimensions={0}, use_global_device_ids=true | all-gather | bytes 143360 | tf_op jit(solution)/shard_map/all_gather | solution.py:102
  (822 shorter events, 411.8 us)
Async XLA Ops:
  7.2 50.8 %all-gather.47.cloned.1.call-start = ((), (), s32[]{:S(2)}) async-start(), calls=%async_computation.5 | async-start | bytes 1310720 | tf_op jit(solution)/shard_map/all_gather | solution.py:50
  8.0 29.6 %copy-start.24 = (bf16[8,1024]{1,0:T(8,128)(2,1)}, bf16[8,1024]{1,0:T(8,128)(2,1)S(1)}, u32[]{:S(2)}) copy-start(bf16[8,1024]{1,0:T(8,128)(2,1)S(1)} %convert_element_type.554) | copy-start | bytes 49156
  28.8 64.0 %all-gather.65.cloned.1.call-start = ((), (), s32[]{:S(2)}) async-start(), calls=%async_computation.14 | async-start | bytes 2621440 | tf_op jit(solution)/shard_map/all_gather | solution.py:31
  31.7 5.9 copy-start.37
  34.1 191.9 %copy-start.28 = (f32[384,16]{0,1:T(8,128)}, f32[384,16]{0,1:T(8,128)S(1)}, u32[]{:S(2)}) copy-start(f32[384,16]{0,1:T(8,128)S(1)} %get-tuple-element.967) | copy-start | bytes 73732
  34.3 3.3 copy-start.63
  35.8 142.1 %copy-start.29 = (f32[384,16]{0,1:T(8,128)}, f32[384,16]{0,1:T(8,128)S(1)}, u32[]{:S(2)}) copy-start(f32[384,16]{0,1:T(8,128)S(1)} %get-tuple-element.969) | copy-start | bytes 73732
  44.0 148.0 %all-gather.49.cloned.1.call-start = ((), (), s32[]{:S(2)}) async-start(), calls=%async_computation.6 | async-start | bytes 3145728 | tf_op jit(solution)/shard_map/all_gather | solution.py:50
  58.0 137.2 %all-gather.45.cloned.1.call-start = ((), (), s32[]{:S(2)}) async-start(), calls=%async_computation.4 | async-start | bytes 2621440 | tf_op jit(solution)/shard_map/all_gather | solution.py:31
  64.9 30.4 %copy-start.81 = (f32[16]{0:T(128)}, f32[16]{0:T(128)S(1)}, u32[]{:S(2)}) copy-start(f32[16]{0:T(128)S(1)} %get-tuple-element.1087) | copy-start | bytes 196
  64.9 30.4 %copy-start.83 = (f32[16]{0:T(128)}, f32[16]{0:T(128)S(1)}, u32[]{:S(2)}) copy-start(f32[16]{0:T(128)S(1)} %get-tuple-element.1088) | copy-start | bytes 196
  64.9 30.4 %copy-start.85 = (f32[16]{0:T(128)}, f32[16]{0:T(128)S(1)}, u32[]{:S(2)}) copy-start(f32[16]{0:T(128)S(1)} %get-tuple-element.1089) | copy-start | bytes 196
  65.5 29.9 %copy-start.73 = (f32[16]{0:T(128)}, f32[16]{0:T(128)S(1)}, u32[]{:S(2)}) copy-start(f32[16]{0:T(128)S(1)} %get-tuple-element.1081) | copy-start | bytes 196
  95.4 115.0 %all-gather.51.cloned.1.call-start = ((), (), s32[]{:S(2)}) async-start(), calls=%async_computation.7 | async-start | bytes 2113536 | tf_op jit(solution)/shard_map/all_gather | solution.py:288
  96.0 158.7 %all-gather.67.cloned.1.call-start = ((), (), s32[]{:S(2)}) async-start(), calls=%async_computation.15 | async-start | bytes 1310720 | tf_op jit(solution)/shard_map/all_gather | solution.py:67
  210.4 5.0 copy-start.4
  210.4 5.0 copy-start.10
  249.8 103.7 %all-to-all-start = ((f32[16,8,1,8,1024]{4,3,1,2,0:T(8,128)}), f32[16,8,1,8,1024]{4,3,1,2,0:T(8,128)}, u32[]{:S(2)}, u32[]{:S(2)}) async-start(f32[16,8,1,8,1024]{4,3,1,2,0:T(8,128)} %copy.198), calls=%async_computation | async-start | bytes 8388608 | tf_op jit(solution)/shard_map/all_to_all | solution.py:90
  254.3 86.7 %all-gather.53.cloned.1.call-start = ((), (), s32[]{:S(2)}) async-start(), calls=%async_computation.8 | async-start | bytes 1310720 | tf_op jit(solution)/shard_map/all_gather | solution.py:67
  341.0 3.3 copy-start.74
  341.1 3.3 copy-start.82
  344.0 4.0 copy-start.26
  353.5 12.2 %copy-start.53 = (pred[384]{0:T(512)(128)(4,1)S(1)}, pred[384]{0:T(512)(128)(4,1)}, u32[]{:S(2)}) copy-start(pred[384]{0:T(512)(128)(4,1)} %copy-done.51) | copy-start | bytes 1156
  353.5 12.3 %copy-start.59 = (f32[16]{0:T(128)S(1)}, f32[16]{0:T(128)}, u32[]{:S(2)}) copy-start(f32[16]{0:T(128)} %param.30) | copy-start | bytes 196
  353.5 12.3 %copy-start.65 = (f32[16]{0:T(128)S(1)}, f32[16]{0:T(128)}, u32[]{:S(2)}) copy-start(f32[16]{0:T(128)} %copy-done.63) | copy-start | bytes 196
  353.5 12.3 %copy-start.66 = (f32[16,3]{0,1:T(4,128)S(1)}, f32[16,3]{0,1:T(4,128)}, u32[]{:S(2)}) copy-start(f32[16,3]{0,1:T(4,128)} %slice.1374) | copy-start | bytes 580
  356.7 15.5 %all-to-all-start.1 = ((f32[8,1,1,8,1024]{4,3,2,1,0:T(8,128)}), f32[8,1,1,8,1024]{4,3,2,1,0:T(8,128)S(1)}, u32[]{:S(2)}, u32[]{:S(2)}) async-start(f32[8,1,1,8,1024]{4,3,2,1,0:T(8,128)} %bitcast.88), calls=%async_computation.1 | async-start | bytes 524288 | tf_op jit(solution)/shard_map/all_to_all | solution.py:90
  365.7 136.5 %all-gather.57.cloned.1.call-start = ((), (), s32[]{:S(2)}) async-start(), calls=%async_computation.10 | async-start | bytes 1310720 | tf_op jit(solution)/shard_map/all_gather | solution.py:50
  367.4 83.4 %copy-start.22 = (f32[8,1024]{1,0:T(8,128)S(1)}, f32[8,1024]{1,0:T(8,128)}, u32[]{:S(2)}) copy-start(f32[8,1024]{1,0:T(8,128)} %param.28) | copy-start | bytes 98308
  367.5 83.4 %copy-start.99 = (f32[16]{0:T(128)S(1)}, f32[16]{0:T(128)}, u32[]{:S(2)}) copy-start(f32[16]{0:T(128)} %param.29) | copy-start | bytes 196
  372.2 98.4 %copy-start.20 = (f32[8,1024]{1,0:T(8,128)}, f32[8,1024]{1,0:T(8,128)S(1)}, u32[]{:S(2)}) copy-start(f32[8,1024]{1,0:T(8,128)S(1)} %reduce_sum.600) | copy-start | bytes 98308
  373.5 9.9 %copy-start.44 = (f32[1,1024]{1,0:T(1,128)}, f32[1,1024]{1,0:T(1,128)S(1)}, u32[]{:S(2)}) copy-start(f32[1,1024]{1,0:T(1,128)S(1)} %reshape.1946) | copy-start | bytes 12292
  383.5 87.7 %copy-start.60 = (f32[16]{0:T(128)S(1)}, f32[16]{0:T(128)}, u32[]{:S(2)}) copy-start(f32[16]{0:T(128)} %param.30) | copy-start | bytes 196
  389.3 83.4 %copy-start.39 = (f32[384]{0:T(512)S(1)}, f32[384]{0:T(512)}, u32[]{:S(2)}) copy-start(f32[384]{0:T(512)} %copy-done.37) | copy-start | bytes 4612
  389.3 83.4 %copy-start.54 = (pred[384]{0:T(512)(128)(4,1)S(1)}, pred[384]{0:T(512)(128)(4,1)}, u32[]{:S(2)}) copy-start(pred[384]{0:T(512)(128)(4,1)} %copy-done.51) | copy-start | bytes 1156
  450.9 26.2 %copy-start.25 = (bf16[8,1024]{1,0:T(8,128)(2,1)}, bf16[8,1024]{1,0:T(8,128)(2,1)S(1)}, u32[]{:S(2)}) copy-start(bf16[8,1024]{1,0:T(8,128)(2,1)S(1)} %fusion.376) | copy-start | bytes 49156
  451.4 19.9 %copy-start.69 = (f32[16]{0:T(128)}, f32[16]{0:T(128)S(1)}, u32[]{:S(2)}) copy-start(f32[16]{0:T(128)S(1)} %get-tuple-element.886) | copy-start | bytes 196
  470.7 66.4 %all-gather.69.cloned.1.call-start = ((), (), s32[]{:S(2)}) async-start(), calls=%async_computation.16 | async-start | bytes 2621440 | tf_op jit(solution)/shard_map/all_gather | solution.py:31
  471.2 5.9 copy-start.56
  472.4 4.7 copy-start.33
  472.4 144.1 %copy-start.27 = (f32[384,16]{0,1:T(8,128)}, f32[384,16]{0,1:T(8,128)S(1)}, u32[]{:S(2)}) copy-start(f32[384,16]{0,1:T(8,128)S(1)} %get-tuple-element.963) | copy-start | bytes 73732
  472.6 4.4 copy-start.61
  472.8 149.9 %copy-start.31 = (f32[384,16]{0,1:T(8,128)}, f32[384,16]{0,1:T(8,128)S(1)}, u32[]{:S(2)}) copy-start(f32[384,16]{0,1:T(8,128)S(1)} %get-tuple-element.965) | copy-start | bytes 73732
  486.0 150.1 %all-gather.59.cloned.1.call-start = ((), (), s32[]{:S(2)}) async-start(), calls=%async_computation.11 | async-start | bytes 3145728 | tf_op jit(solution)/shard_map/all_gather | solution.py:50
  502.3 137.0 %all-gather.55.cloned.1.call-start = ((), (), s32[]{:S(2)}) async-start(), calls=%async_computation.9 | async-start | bytes 2621440 | tf_op jit(solution)/shard_map/all_gather | solution.py:31
  509.2 30.4 %copy-start.75 = (f32[16]{0:T(128)}, f32[16]{0:T(128)S(1)}, u32[]{:S(2)}) copy-start(f32[16]{0:T(128)S(1)} %get-tuple-element.1069) | copy-start | bytes 196
  509.2 30.4 %copy-start.77 = (f32[16]{0:T(128)}, f32[16]{0:T(128)S(1)}, u32[]{:S(2)}) copy-start(f32[16]{0:T(128)S(1)} %get-tuple-element.1070) | copy-start | bytes 196
  509.2 30.4 %copy-start.79 = (f32[16]{0:T(128)}, f32[16]{0:T(128)S(1)}, u32[]{:S(2)}) copy-start(f32[16]{0:T(128)S(1)} %get-tuple-element.1071) | copy-start | bytes 196
  509.7 29.9 %copy-start.71 = (f32[16]{0:T(128)}, f32[16]{0:T(128)S(1)}, u32[]{:S(2)}) copy-start(f32[16]{0:T(128)S(1)} %get-tuple-element.1063) | copy-start | bytes 196
  539.6 114.7 %all-gather.61.cloned.1.call-start = ((), (), s32[]{:S(2)}) async-start(), calls=%async_computation.12 | async-start | bytes 2113536 | tf_op jit(solution)/shard_map/all_gather | solution.py:288
  540.2 159.0 %all-gather.71.cloned.1.call-start = ((), (), s32[]{:S(2)}) async-start(), calls=%async_computation.17 | async-start | bytes 1310720 | tf_op jit(solution)/shard_map/all_gather | solution.py:67
  555.9 66.2 %copy-start.43 = (f32[1024]{0:T(1024)S(1)}, f32[1024]{0:T(1024)}, u32[]{:S(2)}) copy-start(f32[1024]{0:T(1024)} %param.32) | copy-start | bytes 12292
  624.0 11.0 %copy-start.101 = (f32[16]{0:T(128)S(1)}, f32[16]{0:T(128)}, u32[]{:S(2)}) copy-start(f32[16]{0:T(128)} %param.31) | copy-start | bytes 196
  666.1 8.8 copy-start.36
  666.1 14.6 %copy-start.35 = (f32[4,1,1024]{2,1,0:T(1,128)S(1)}, f32[4,1,1024]{2,1,0:T(1,128)}, u32[]{:S(2)}) copy-start(f32[4,1,1024]{2,1,0:T(1,128)} %get-tuple-element.916) | copy-start | bytes 49156
  694.4 100.8 %all-to-all-start.2 = ((f32[16,8,1,8,1024]{4,3,1,2,0:T(8,128)}), f32[16,8,1,8,1024]{4,3,1,2,0:T(8,128)}, u32[]{:S(2)}, u32[]{:S(2)}) async-start(f32[16,8,1,8,1024]{4,3,1,2,0:T(8,128)} %copy.220), calls=%async_computation.2 | async-start | bytes 8388608 | tf_op jit(solution)/shard_map/all_to_all | solution.py:90
  698.9 84.9 %all-gather.63.cloned.1.call-start = ((), (), s32[]{:S(2)}) async-start(), calls=%async_computation.13 | async-start | bytes 1310720 | tf_op jit(solution)/shard_map/all_gather | solution.py:67
  795.1 14.1 %copy-start.70 = (f32[16]{0:T(128)S(1)}, f32[16]{0:T(128)}, u32[]{:S(2)}) copy-start(f32[16]{0:T(128)} %copy-done.69) | copy-start | bytes 196
  795.1 14.4 %copy-start.87 = (f32[16]{0:T(128)S(1)}, f32[16]{0:T(128)}, u32[]{:S(2)}) copy-start(f32[16]{0:T(128)} %get-tuple-element.887) | copy-start | bytes 196
  795.1 21.9 %copy-start.45 = (f32[1,1024]{1,0:T(1,128)S(1)}, f32[1,1024]{1,0:T(1,128)}, u32[]{:S(2)}) copy-start(f32[1,1024]{1,0:T(1,128)} %copy-done.44) | copy-start | bytes 12292
  798.3 17.4 %all-to-all-start.3 = ((f32[8,1,1,8,1024]{4,3,2,1,0:T(8,128)}), f32[8,1,1,8,1024]{4,3,2,1,0:T(8,128)S(1)}, u32[]{:S(2)}, u32[]{:S(2)}) async-start(f32[8,1,1,8,1024]{4,3,2,1,0:T(8,128)} %bitcast.244), calls=%async_computation.3 | async-start | bytes 524288 | tf_op jit(solution)/shard_map/all_to_all | solution.py:90
  809.6 93.6 %copy-start.21 = (f32[8,1024]{1,0:T(8,128)S(1)}, f32[8,1024]{1,0:T(8,128)}, u32[]{:S(2)}) copy-start(f32[8,1024]{1,0:T(8,128)} %copy-done.20) | copy-start | bytes 98308
  809.6 93.6 %copy-start.23 = (f32[8,1024]{1,0:T(8,128)S(1)}, f32[8,1024]{1,0:T(8,128)}, u32[]{:S(2)}) copy-start(f32[8,1024]{1,0:T(8,128)} %param.28) | copy-start | bytes 98308
  815.7 89.1 %copy-start.100 = (f32[16]{0:T(128)S(1)}, f32[16]{0:T(128)}, u32[]{:S(2)}) copy-start(f32[16]{0:T(128)} %bitcast_subtract_fusion.3) | copy-start | bytes 196
  (57 other events, 157.8 us)
Sparse Core Ops, SparseCore 0:
  28.9 29.0 all-gather.46
  59.6 33.0 all-gather.64
  94.4 13.7 all-gather.48
  109.7 31.4 all-gather.44
  144.1 65.9 all-gather.50
  226.1 22.2 all-gather.66
  257.0 40.5 all-gather.52
  470.8 31.3 all-gather.56
  503.9 33.0 all-gather.68
  538.6 13.7 all-gather.58
  554.0 31.4 all-gather.54
  588.3 65.9 all-gather.60
  669.2 24.3 all-gather.70
  701.6 40.9 all-gather.62
where the time goes:
time: 929 us; the launch traced here: 913 us
  matrix products  267 us (29%)
  blocking collectives  161 us (17%)
  other arithmetic  138 us (15%)
  local copies, waits for them, and re-layouts  118 us (13%)
  between operations  101 us (11%)
  waiting for transfers between devices  97 us (10%)
  starting transfers between devices  30.4 us (3%)
    dot_general x96, matrix products, one_head(): return jnp.dot(decay_grid * scores, head_scaled, precision=highest)  219 us
    all_gather x8, blocking collectives, collected_together(): both, at, found = (lax.all_gather(jnp.concatenate(lines), axis), 0, {})  68.1 us
    all_gather x4, waiting for transfers between devices, entering_2(): pieces = jax.tree.map(lambda part: lax.all_gather(part, axis), so_far)  54.6 us
    dynamic_update_slice x32, other arithmetic, mix_block(): lax.map(one_head, (decay_sum.T, jnp.transpose(scaled, (1, 0, 2))))  40.7 us
    all_gather x4, blocking collectives, stacked_from(): tiles = lax.all_gather(tiles, axes[k], axis=0, tiled=True)  40.1 us
    all_gather x4, waiting for transfers between devices, stacked_from(): tiles = lax.all_gather(tiles, axes[k], axis=0, tiled=True)  30.1 us
    all_gather x4, blocking collectives, entering_2(): pieces = jax.tree.map(lambda part: lax.all_gather(part, axis), so_far)  29.4 us
    all_to_all x4, starting transfers between devices, sent_and_summed(): tiles = lax.all_to_all(split_up(array, dim, count), axis, 0, 0, tiled=True)  29 us
  transfers between devices with their start and end apart: 18, of which 6 were waited for; matrix products, arithmetic and copies ran while one was open for 50% of the time, Pallas kernels for 0%

commit v1 on v0

v1 whole, which is shorter than its diff:
```python
import jax
import jax.numpy as jnp
from jax import lax
from jax.experimental import pallas as pl
from jax.experimental.pallas import tpu as pltpu
from jax.sharding import PartitionSpec as P

STEPS = 2
DP, SEQ = "dp", "seq"
N_DP, N_SEQ, N_Y = 8, 16, 4
TOK, WIDE, STATE, HEADS, HEAD = 384, 1024, 128, 16, 64
CHUNK, CHUNKS, PAIRS = 128, 3, 8
HALF = WIDE // 2

norm_floor = 1.0
clip_limit = 1.0
learn_rate = 8.0
f32, bf16 = jnp.float32, jnp.bfloat16
highest = lax.Precision.HIGHEST


def dot(a, b):
    return jnp.dot(a, b, preferred_element_type=f32)


def dot_tn(a, b):
    return lax.dot_general(a, b, (((0,), (0,)), ((), ())), preferred_element_type=f32)


def dot_nt(a, b):
    return lax.dot_general(a, b, (((1,), (1,)), ((), ())), preferred_element_type=f32)


def iota(shape, dim):
    return lax.broadcasted_iota(jnp.int32, shape, dim)


def three_parts(v):
    high = v.astype(bf16).astype(f32)
    rest = v - high
    mid = rest.astype(bf16).astype(f32)
    low = rest - mid
    group = (iota(v.shape, 1) >> 4) & 3
    zero = jnp.zeros_like(v)
    return jnp.where(
        group == 0, high, jnp.where(group == 1, mid, jnp.where(group == 2, low, zero))
    ).astype(bf16)


def blocks_of(rows):
    left = rows[:, :HALF].reshape(N_SEQ, 1, 8, HALF)
    right = rows[:, HALF:].reshape(N_SEQ, 1, 8, HALF)
    return jnp.concatenate([left, right], axis=1).reshape(N_SEQ, 16, HALF)


def rows_of(blocks):
    count = blocks.shape[0]
    split = blocks.reshape(count, 2, 8, HALF)
    return split[:, 0].reshape(count * 8, HALF), split[:, 1].reshape(count * 8, HALF)


def kernel(
    x_ref, z_ref, bc_ref, raw_ref, ids_ref, cnt_ref, tgt_ref, w_ref, dec_in, bias_in, skip_in, gain_in,
    loss_out, w_out, dec_out, bias_out, skip_out, gain_out,
    ex, red, tri, par, gain, wown,
    rawt, wid, dec_s, ent, tail, chain, fcol, sc,
    xw, yin, eexp, silu, gstate, hst, apart, normb, ogb, gb, zin, ds1, accs,
    hs, hr, hp, hi, gs, gr, gp, gi, cs, cr,
    agb, wfull, wgp, pr, sb, rb,
    sa, sar, sb2, sbr, ta, tar, tb, tbr,
    s_send, s_recv, s_ag, s_agr, s_fs, s_fr, s_ps, s_pr, s_rs, s_rr,
):
    dp, seq = lax.axis_index(DP), lax.axis_index(SEQ)
    yy, core = dp // 2, dp % 2
    partner = dp + 1 - 2 * core
    own_q = yy * N_SEQ + seq
    own_b = dp * N_SEQ + seq
    MESH = pl.DeviceIdType.MESH

    def at(d, s):
        return {DP: d, SEQ: s}

    def remote(src, dst, ss, rs, d, s):
        return pltpu.make_async_remote_copy(
            src_ref=src, dst_ref=dst, send_sem=ss, recv_sem=rs, device_id=at(d, s), device_id_type=MESH
        )

    barrier = pltpu.get_barrier_semaphore()

    def greet_same(k, carry):
        q = (own_q + k) % 64
        pl.semaphore_signal(barrier, 1, device_id=at((q // 16) * 2 + core, q % 16), device_id_type=MESH)
        return carry

    lax.fori_loop(1, 64, greet_same, 0)

    def greet_other(k, carry):
        pl.semaphore_signal(barrier, 1, device_id=at(k * 2 + 1 - core, seq), device_id_type=MESH)
        return carry

    lax.fori_loop(0, N_Y, greet_other, 0)

    row = iota((CHUNK, WIDE), 0)
    col = iota((CHUNK, WIDE), 1)
    ex[...] = jnp.where(((row & 15) == (col >> 6)) & (row < 48), 1.0, 0.0).astype(bf16)
    rrow = iota((WIDE, 128), 0)
    rcol = iota((WIDE, 128), 1)
    red[...] = jnp.where((rrow >> 6) == (rcol & 15), 1.0, 0.0).astype(bf16)
    ti, tj = iota((CHUNK, CHUNK), 0), iota((CHUNK, CHUNK), 1)
    tri[...] = jnp.where(ti >= tj, 1.0, 0.0)
    rep = jnp.where(iota((HEADS, 128), 0) == (iota((HEADS, 128), 1) & 15), 1.0, 0.0)

    def tiled(ref):
        return jnp.dot(jnp.broadcast_to(ref[...], (8, HEADS)), rep, precision=highest, preferred_element_type=f32)

    par[0] = tiled(dec_in)
    par[1] = tiled(bias_in)
    par[2] = tiled(skip_in)
    gain[...] = gain_in[...]
    wown[...] = w_ref[...]
    rawt[...] = jnp.dot(raw_ref[...], rep, precision=highest, preferred_element_type=f32)

    def expand(v):
        return dot(three_parts(v), ex[...])

    def head_sum(v):
        high = v.astype(bf16)
        low = (v - high.astype(f32)).astype(bf16)
        return dot(high, red[...]) + dot(low, red[...])

    lane = iota((1, 128), 1)
    low_half = jnp.where(lane < HEAD, 1.0, 0.0).astype(bf16)
    high_half = jnp.where(lane < HEAD, 0.0, 1.0).astype(bf16)

    total = cnt_ref[0]
    for k in range(1, N_DP):
        total = total + cnt_ref[k]
    total_f = total.astype(f32)
    own_count = cnt_ref[dp]

    def rows(c):
        return pl.ds(pl.multiple_of(c * CHUNK, CHUNK), CHUNK)

    def prepare(c, carry):
        flag = jnp.where(ids_ref[0:1, rows(c)] == 0, 1.0, 0.0)
        flag_col = jnp.broadcast_to(flag, (CHUNK, CHUNK)).T
        seg = dot(tri[...], flag_col)
        seg_row = seg.T
        fcol[c] = seg
        scores = dot_nt(bc_ref[rows(c), STATE:], bc_ref[rows(c), :STATE])
        sc[c] = jnp.where((seg == seg_row) & (ti >= tj), scores, 0.0)
        return carry

    lax.fori_loop(0, CHUNKS, prepare, 0)

    def ag_start():
        block = jnp.concatenate([wown[:, :HALF], wown[:, HALF:]], axis=0).astype(bf16)
        agb[own_b] = block

        def send(k, carry):
            q = (own_q + k) % 64
            remote(agb.at[own_b], agb.at[own_b], s_ag, s_agr.at[yy], (q // 16) * 2 + core, q % 16).start()
            return carry

        lax.fori_loop(1, 64, send, 0)

    def ag_finish():
        copies = []
        for k in range(N_Y):
            y_k = (yy + k) % N_Y
            first = (y_k * 2 + core) * N_SEQ
            count = 15 if k == 0 else 16
            piece = agb.at[pl.ds(first, count)]
            remote(piece, piece, s_ag, s_agr.at[y_k], partner, seq).wait_recv()
            whole = agb.at[pl.ds(first, N_SEQ)]
            copy = remote(whole, whole, s_fs.at[k], s_fr.at[k], partner, seq)
            copy.start()
            copies.append(copy)
        for k in range(N_Y):
            y_k = (yy + k) % N_Y
            other = (y_k * 2 + 1 - core) * N_SEQ
            piece = agb.at[pl.ds(other, N_SEQ)]
            remote(piece, piece, s_fs.at[k], s_fr.at[k], partner, seq).wait_recv()
        sent = agb.at[pl.ds(0, 63)]
        remote(sent, sent, s_ag, s_agr.at[0], partner, seq).wait_send()
        for copy in copies:
            copy.wait_send()

        def unpack(d, carry):
            left, right = rows_of(agb[pl.ds(d * N_SEQ, N_SEQ)].astype(f32))
            wfull[rows(d), :HALF] = left.astype(bf16)
            wfull[rows(d), HALF:] = right.astype(bf16)
            return carry

        lax.fori_loop(0, N_DP, unpack, 0)

    def exchange_start(src, dst, n):
        def send(k, carry):
            peer = (seq + k) % N_SEQ
            remote(src.at[peer], dst.at[seq], s_send.at[n], s_recv.at[n], dp, peer).start()
            return carry

        lax.fori_loop(1, N_SEQ, send, 0)
        dst[seq] = src[seq]

    def spread_start(src, dst, n):
        def send(k, carry):
            peer = (seq + k) % N_SEQ
            remote(src, dst.at[seq], s_send.at[n], s_recv.at[n], dp, peer).start()
            return carry

        lax.fori_loop(1, N_SEQ, send, 0)
        dst[seq] = src[...]

    def cross_start(src, dst, n):
        def send(k, carry):
            peer = (dp + k) % N_DP
            remote(src, dst.at[dp], s_send.at[n], s_recv.at[n], peer, seq).start()
            return carry

        lax.fori_loop(1, N_DP, send, 0)
        dst[dp] = src[...]

    def recv_wait(dst, n, count):
        piece = dst.at[pl.ds(0, count)]
        remote(piece, piece, s_send.at[n], s_recv.at[n], partner, seq).wait_recv()

    def send_wait(dst, n, count):
        piece = dst.at[pl.ds(0, count)]
        remote(piece, piece, s_send.at[n], s_recv.at[n], partner, seq).wait_send()

    def one_step(step, losses):
        dec_t, bias_t, skip_t = par[0, 0:1], par[1, 0:1], par[2, 0:1]
        rate = jnp.exp(dec_t)

        hst[0] = jnp.zeros((STATE, WIDE), f32)

        def begin(c, carried):
            seg = fcol[c]
            pre = rawt[rows(c)] + bias_t
            u = jnp.exp(-jnp.abs(pre))
            v = 1.0 + u
            log1p = jnp.where(v == 1.0, u, jnp.log(v) * u / jnp.where(v == 1.0, 1.0, v - 1.0))
            width = jnp.maximum(pre, 0.0) + log1p
            s = jnp.dot(tri[...], -rate * width, precision=highest, preferred_element_type=f32)
            last = s[CHUNK - 1 : CHUNK]
            seg_last = seg[CHUNK - 1 : CHUNK]
            entering = jnp.exp(s) * jnp.where(seg == 0.0, 1.0, 0.0)
            leaving = jnp.exp(last - s) * jnp.where(seg == seg_last, 1.0, 0.0)
            through = jnp.exp(last) * jnp.where(seg_last == 0.0, 1.0, 0.0)
            wid[rows(c)] = width
            dec_s[rows(c)] = s
            tail[rows(c)] = leaving
            eexp[rows(c)] = expand(entering)
            chain[c] = expand(jnp.broadcast_to(through, (8, 128)))
            scaled = x_ref[rows(c)].astype(f32) * expand(width)
            xw[rows(c)] = scaled.astype(bf16)
            weighted = (scaled * expand(leaving)).astype(bf16)
            added = dot_tn(bc_ref[rows(c), :STATE], weighted)
            gstate[c] = added
            hst[0] = chain[c][0:1] * hst[0] + added
            return carried * through

        carried = lax.fori_loop(0, CHUNKS, begin, jnp.ones((1, 128), f32))
        wide8 = jnp.broadcast_to(carried, (8, 128))
        sub8, lane8 = iota((8, 128), 0), iota((8, 128), 1)
        even = jnp.sum(jnp.where(lane8 == 2 * sub8, wide8, 0.0), axis=1, keepdims=True)
        odd = jnp.sum(jnp.where(lane8 == 2 * sub8 + 1, wide8, 0.0), axis=1, keepdims=True)
        cs[...] = jnp.where(lane8 < HEAD, even, odd)

        def to_blocks(state, out):
            for r in range(8):
                for h in range(2):
                    out[2 * r + h] = state[16 * r : 16 * r + 16, HALF * h : HALF * (h + 1)].astype(bf16)

        to_blocks(hst[0], hs)

        @pl.when(step == 0)
        def _():
            pl.semaphore_wait(barrier, 67)

        exchange_start(hs, hr, 0)
        spread_start(cs, cr, 1)

        @pl.when(step == 0)
        def _():
            ag_start()

        def inside(c, carry):
            s = dec_s[rows(c)]
            s_t = s.T
            scores = sc[c]
            for p in range(PAIRS):
                parts = []
                for h in (2 * p, 2 * p + 1):
                    gap = jnp.minimum(s[:, h : h + 1] - s_t[h : h + 1, :], 0.0)
                    parts.append((jnp.exp(gap) * scores).astype(bf16))
                mine = xw[rows(c), 128 * p : 128 * (p + 1)]
                both = jnp.concatenate([mine * low_half, mine * high_half], axis=0)
                yin[rows(c), 128 * p : 128 * (p + 1)] = dot(jnp.concatenate(parts, axis=1), both)
            return carry

        lax.fori_loop(0, CHUNKS, inside, 0)

        half = seq % 2

        def carry_rows(i):
            return [cr[i, pl.ds(4 * half + m, 1), :] for m in range(4)]

        recv_wait(hr, 0, 15)
        recv_wait(cr, 1, 15)

        def forward(i, state):
            factors = carry_rows(i)
            out = []
            for m in range(4):
                lanes = slice(128 * m, 128 * (m + 1))
                hp[i, :, lanes] = state[m].astype(bf16)
                out.append(factors[m] * state[m] + hr[i, :, lanes].astype(f32))
            return tuple(out)

        zeros4 = tuple(jnp.zeros((16, 128), f32) for _ in range(4))
        lax.fori_loop(0, N_SEQ, forward, zeros4)
        exchange_start(hp, hi, 2)
        ag_finish()
        recv_wait(hi, 2, 15)
        for r in range(8):
            for h in range(2):
                hst[0, 16 * r : 16 * r + 16, HALF * h : HALF * (h + 1)] = hi[2 * r + h].astype(f32)

        skip_e = expand(jnp.broadcast_to(skip_t, (8, 128)))[0:1]
        gain_e = gain[...]
        scale = 2.0 / (WIDE * total_f)
        accs[...] = jnp.zeros(accs.shape, f32)

        def mix(c, loss):
            state = hst[c]
            b_c, c_c = bc_ref[rows(c), :STATE], bc_ref[rows(c), STATE:]
            y_sum = yin[rows(c)] + eexp[rows(c)] * dot(c_c, state.astype(bf16))
            x_f = x_ref[rows(c)].astype(f32)
            z_f = z_ref[rows(c)].astype(f32)
            act = z_f / (1.0 + jnp.exp(-z_f))
            gated = (y_sum + skip_e * x_f) * act
            inv = lax.rsqrt(jnp.sum(gated * gated, axis=1, keepdims=True) * (1.0 / WIDE) + norm_floor)
            normed = (gated * gain_e * inv).astype(bf16)
            normb[rows(c)] = normed
            res = dot(normed, wfull[...]) - tgt_ref[rows(c)].astype(f32)
            position = seq * TOK + c * CHUNK + iota((CHUNK, 1), 0)
            scored = jnp.where(position < own_count, 1.0, 0.0)
            loss = loss + jnp.sum(jnp.sum(res * res, axis=1, keepdims=True) * scored, axis=0, keepdims=True)
            og = (res * (scored * scale)).astype(bf16)
            ogb[rows(c)] = og
            d_norm = dot_nt(og, wfull[...])
            d_gr = d_norm * gated * inv
            accs[0] += jnp.sum(d_gr.reshape(16, 8, WIDE), axis=0)
            inner = jnp.sum(d_gr * gain_e, axis=1, keepdims=True) * (1.0 / WIDE)
            d_gated = inv * (gain_e * d_norm - gated * (inv * inner))
            g = d_gated * act
            g_b = g.astype(bf16)
            gb[rows(c)] = g_b
            accs[1] += jnp.sum((g * x_f).reshape(16, 8, WIDE), axis=0)
            ds1[rows(c)] = head_sum(g_b.astype(f32) * y_sum)
            apart[c] = dot_tn(c_c, (g * eexp[rows(c)]).astype(bf16))
            hst[c + 1] = chain[c][0:1] * state + gstate[c]
            return loss

        loss = lax.fori_loop(0, CHUNKS, mix, jnp.zeros((1, 1), f32))
        entry = apart[0] + chain[0][0:1] * (apart[1] + chain[1][0:1] * apart[2])
        to_blocks(entry, gs)
        exchange_start(gs, gr, 3)
        gain_g = jnp.sum(accs[0], axis=0, keepdims=True)
        for r in range(8):
            sa[r : r + 1, :] = gain_g[:, 128 * r : 128 * (r + 1)]
        skip_g = head_sum(jnp.broadcast_to(jnp.sum(accs[1], axis=0, keepdims=True), (8, WIDE)))
        sub = iota((8, 128), 0)
        sa[8:16, :] = jnp.where(sub == 0, skip_g, jnp.where(sub == 1, jnp.broadcast_to(loss, (8, 128)), 0.0))
        spread_start(sa, sar, 4)

        def grad_rows(d):
            lanes = pl.ds(pl.multiple_of(d * 128, 128), 128)
            return blocks_of(dot_tn(normb[:, lanes], ogb[...]))

        for k in range(N_Y):
            y_k = (yy + k) % N_Y
            d = y_k * 2 + 1 - core
            wgp[k] = grad_rows(d).astype(bf16)
            remote(wgp.at[k], pr.at[k], s_ps.at[k], s_pr.at[k], partner, seq).start()
        for k in range(N_Y):
            y_k = (yy + k) % N_Y
            d = y_k * 2 + core
            mine = grad_rows(d)
            remote(wgp.at[k], pr.at[k], s_ps.at[k], s_pr.at[k], partner, seq).wait_recv()
            sb[pl.ds(y_k * N_SEQ, N_SEQ)] = (mine + pr[k].astype(f32)).astype(bf16)

            def send(j, carry):
                s = (seq + j) % N_SEQ
                remote(sb.at[y_k * N_SEQ + s], rb.at[own_q], s_rs, s_rr, d, s).start()
                return carry

            lax.fori_loop(1 if k == 0 else 0, N_SEQ, send, 0)
        rb[own_q] = sb[own_q]

        recv_wait(gr, 3, 15)

        def backward(n, state):
            i = N_SEQ - 1 - n
            factors = carry_rows(i)
            out = []
            for m in range(4):
                lanes = slice(128 * m, 128 * (m + 1))
                gp[i, :, lanes] = state[m].astype(bf16)
                out.append(factors[m] * state[m] + gr[i, :, lanes].astype(f32))
            return tuple(out)

        lax.fori_loop(0, N_SEQ, backward, zeros4)
        exchange_start(gp, gi, 5)

        def inside_back(c, carry):
            s = dec_s[rows(c)]
            s_t = s.T
            scores = sc[c].T
            for p in range(PAIRS):
                parts = []
                for h in (2 * p, 2 * p + 1):
                    gap = jnp.minimum(s_t[h : h + 1, :] - s[:, h : h + 1], 0.0)
                    parts.append((jnp.exp(gap) * scores).astype(bf16))
                mine = gb[rows(c), 128 * p : 128 * (p + 1)]
                both = jnp.concatenate([mine * low_half, mine * high_half], axis=0)
                zin[rows(c), 128 * p : 128 * (p + 1)] = dot(jnp.concatenate(parts, axis=1), both)
            return carry

        lax.fori_loop(0, CHUNKS, inside_back, 0)

        def summed(ref, count):
            value = ref[0]
            for k in range(1, count):
                value = value + ref[k]
            return value

        recv_wait(sar, 4, 15)
        sb2[...] = summed(sar, N_SEQ)
        cross_start(sb2, sbr, 6)

        recv_wait(gi, 5, 15)
        for r in range(8):
            for h in range(2):
                apart[3, 16 * r : 16 * r + 16, HALF * h : HALF * (h + 1)] = gi[2 * r + h].astype(f32)

        def back(n, sums):
            dec_g, bias_g = sums
            c = CHUNKS - 1 - n
            after = apart[3]
            width = wid[rows(c)]
            z_t = dot(bc_ref[rows(c), :STATE], after.astype(bf16))
            z_all = zin[rows(c)] + expand(tail[rows(c)]) * z_t
            q2 = head_sum(xw[rows(c)].astype(f32) * z_all)
            ends = jnp.sum((after * hst[c + 1]).reshape(16, 8, WIDE), axis=0)
            end_h = jnp.sum(head_sum(ends), axis=0, keepdims=True)
            d_s = ds1[rows(c)] - q2
            d_a = lax.dot_general(
                tri[...], d_s, (((0,), (0,)), ((), ())), precision=highest, preferred_element_type=f32
            ) + end_h
            d_w = q2 / width - rate * d_a
            pre = rawt[rows(c)] + bias_t
            sig = 1.0 / (1.0 + jnp.exp(-pre))
            dec_g = dec_g - jnp.sum(d_a * (rate * width), axis=0, keepdims=True)
            bias_g = bias_g + jnp.sum(d_w * sig, axis=0, keepdims=True)
            apart[3] = apart[c] + chain[c][0:1] * after
            return dec_g, bias_g

        zero_row = jnp.zeros((1, 128), f32)
        dec_g, bias_g = lax.fori_loop(0, CHUNKS, back, (zero_row, zero_row))

        recv_wait(sbr, 6, 7)
        sums_a = summed(sbr, N_DP)

        got = rb.at[pl.ds(0, 63)]
        remote(got, got, s_rs, s_rr, partner, seq).wait_recv()

        def add_up(q, value):
            return value + rb[q].astype(f32)

        grad = lax.fori_loop(0, 64, add_up, jnp.zeros((16, HALF), f32))
        square = jnp.sum(jnp.sum(grad * grad, axis=1, keepdims=True), axis=0, keepdims=True)
        ta[...] = jnp.where(
            sub == 0, dec_g, jnp.where(sub == 1, bias_g, jnp.where(sub == 2, jnp.broadcast_to(square, (8, 128)), 0.0))
        )
        spread_start(ta, tar, 7)
        recv_wait(tar, 7, 15)
        tb[...] = summed(tar, N_SEQ)
        cross_start(tb, tbr, 8)
        recv_wait(tbr, 8, 7)
        sums_b = summed(tbr, N_DP)

        dec_g, bias_g, squares = sums_b[0:1], sums_b[1:2], sums_b[2:3]
        gain_rows, skip_g, loss_all = sums_a[0:8], sums_a[8:9], sums_a[9:10]
        small = jnp.sum(
            jnp.where(lane < HEADS, dec_g * dec_g + bias_g * bias_g + skip_g * skip_g, 0.0), axis=1, keepdims=True
        )
        gains = jnp.sum(jnp.sum(gain_rows * gain_rows, axis=1, keepdims=True), axis=0, keepdims=True)
        norm = jnp.sqrt(squares + (small + gains))
        move = learn_rate * (clip_limit / jnp.maximum(norm, clip_limit))
        par[0] = jnp.broadcast_to(dec_t - move * dec_g, (8, 128))
        par[1] = jnp.broadcast_to(bias_t - move * bias_g, (8, 128))
        par[2] = jnp.broadcast_to(skip_t - move * skip_g, (8, 128))
        for r in range(8):
            lanes = slice(128 * r, 128 * (r + 1))
            gain[:, lanes] = gain[:, lanes] - move * gain_rows[r : r + 1]
        move_w = jnp.broadcast_to(move[:, 0:1], (8, HALF))
        wown[:, :HALF] = wown[:, :HALF] - move_w * grad[0:8]
        wown[:, HALF:] = wown[:, HALF:] - move_w * grad[8:16]

        send_wait(hr, 0, 15)
        send_wait(cr, 1, 15)
        send_wait(hi, 2, 15)
        send_wait(gr, 3, 15)
        send_wait(sar, 4, 15)
        send_wait(gi, 5, 15)
        send_wait(sbr, 6, 7)
        send_wait(tar, 7, 15)
        send_wait(tbr, 8, 7)
        for k in range(N_Y):
            remote(wgp.at[k], pr.at[k], s_ps.at[k], s_pr.at[k], partner, seq).wait_send()
        remote(got, got, s_rs, s_rr, partner, seq).wait_send()

        @pl.when(step == 0)
        def _():
            ag_start()

        step_loss = loss_all[:, 0:1] * (1.0 / WIDE) / total_f
        return jnp.where(iota((1, STEPS), 1) == step, step_loss, losses)

    losses = lax.fori_loop(0, STEPS, one_step, jnp.zeros((1, STEPS), f32))
    loss_out[...] = losses
    w_out[...] = wown[...]
    dec_out[...] = par[0, 0:1, :HEADS]
    bias_out[...] = par[1, 0:1, :HEADS]
    skip_out[...] = par[2, 0:1, :HEADS]
    gain_out[...] = gain[...]


def per_device(x, z, bc, raw, ids, counts, target, weight, dec, bias, skip, gain):
    vmem = pl.BlockSpec(memory_space=pltpu.VMEM)
    smem = pl.BlockSpec(memory_space=pltpu.SMEM)
    dma = pltpu.SemaphoreType.DMA
    shape = jax.ShapeDtypeStruct
    v = pltpu.VMEM
    rows_f = v((TOK, 128), f32)
    wide_f = v((TOK, WIDE), f32)
    wide_b = v((TOK, WIDE), bf16)
    states = v((CHUNKS + 1, STATE, WIDE), f32)
    sixteen = v((N_SEQ, 16, HALF), bf16)
    outs = pl.pallas_call(
        kernel,
        out_shape=(
            shape((1, STEPS), f32), shape((8, WIDE), f32), shape((1, HEADS), f32), shape((1, HEADS), f32),
            shape((1, HEADS), f32), shape((1, WIDE), f32),
        ),
        in_specs=[vmem] * 5 + [smem] + [vmem] * 6,
        out_specs=(vmem,) * 6,
        scratch_shapes=[
            v((128, WIDE), bf16), v((WIDE, 128), bf16), v((CHUNK, CHUNK), f32), v((3, 8, 128), f32), v((1, WIDE), f32),
            v((8, WIDE), f32),
            rows_f, rows_f, rows_f, v((8, 128), f32), rows_f, v((CHUNKS, 8, WIDE), f32),
            v((CHUNKS, CHUNK, CHUNK), f32), v((CHUNKS, CHUNK, CHUNK), f32),
            wide_b, wide_f, wide_f, v((8, 128), f32), v((CHUNKS, STATE, WIDE), f32), states, states, wide_b, wide_b, wide_b,
            wide_f, rows_f, v((2, 8, WIDE), f32),
            sixteen, sixteen, sixteen, sixteen, sixteen, sixteen, sixteen, sixteen, v((8, 128), f32),
            v((N_SEQ, 8, 128), f32),
            v((128, 16, HALF), bf16), v((WIDE, WIDE), bf16), v((N_Y, N_SEQ, 16, HALF), bf16),
            v((N_Y, N_SEQ, 16, HALF), bf16), v((64, 16, HALF), bf16), v((64, 16, HALF), bf16),
            v((16, 128), f32), v((N_SEQ, 16, 128), f32), v((16, 128), f32), v((N_DP, 16, 128), f32),
            v((8, 128), f32), v((N_SEQ, 8, 128), f32), v((8, 128), f32), v((N_DP, 8, 128), f32),
            dma((9,)), dma((9,)), dma, dma((N_Y,)), dma((N_Y,)), dma((N_Y,)), dma((N_Y,)), dma((N_Y,)), dma, dma,
        ],
        compiler_params=pltpu.CompilerParams(
            collective_id=0, has_side_effects=True, vmem_limit_bytes=62 * 1024 * 1024
        ),
    )(
        x[0], z[0], bc[0], raw[0], ids, counts, target[0], weight,
        dec.reshape(1, HEADS), bias.reshape(1, HEADS), skip.reshape(1, HEADS), gain.reshape(1, WIDE),
    )
    losses, weight, dec, bias, skip, gain = outs
    return (
        losses.reshape(STEPS), weight, dec.reshape(HEADS), bias.reshape(HEADS), skip.reshape(HEADS), gain.reshape(WIDE)
    )


def solution(mesh):
    tokens = P(DP, SEQ, None)
    return jax.shard_map(
        per_device,
        mesh=mesh,
        in_specs=(
            tokens, tokens, tokens, tokens, P(DP, SEQ), P(), tokens, P((DP, SEQ), None), P(), P(), P(), P(),
        ),
        out_specs=(P(), P((DP, SEQ), None), P(), P(), P(), P()),
        check_vma=False,
    )
```

time: 929 us -> 153 us (0.16); the launches traced: 913 us -> 152 us
  matrix products: 267 us -> 0 us
  blocking collectives: 161 us -> 0 us
  Pallas kernels: 0 us -> 146 us
  other arithmetic: 138 us -> 0 us
  local copies, waits for them, and re-layouts: 118 us -> 6.17 us
  between operations: 101 us -> 0.66 us
  waiting for transfers between devices: 97 us -> 0 us
  starting transfers between devices: 30.4 us -> 0 us
    dot_general x111 -> x0, matrix products: 267 us -> none  [the longest x96 219 us: one_head(): return jnp.dot(decay_grid * scores, head_scaled, precision=highest)]
    all_gather x20 -> x0, blocking collectives: 161 us -> none  [the longest x8 68.1 us: collected_together(): both, at, found = (lax.all_gather(jnp.concatenate(lines), axis), 0, {})]
    pallas_call x0 -> x1, Pallas kernels: none -> 146 us  [per_device(): pl.pallas_call(kernel, out_shape=(shape((1, STEPS), f32), shape((8, WIDE)...]
    all_gather x14 -> x0, waiting for transfers between devices: 84.9 us -> none  [the longest x4 54.6 us: entering_2(): pieces = jax.tree.map(lambda part: lax.all_gather(part, axis), so_far)]
    dynamic_update_slice x32 -> x0, other arithmetic: 40.7 us -> none  [mix_block(): lax.map(one_head, (decay_sum.T, jnp.transpose(scaled, (1, 0, 2))))]
    reduce_sum x32 -> x0, other arithmetic: 37.1 us -> none  [the longest x2 7.04 us: per_device(): carry_grad = jnp.sum(after_grad * state_in, axis=(1, 2))]
    mul x18 -> x0, local copies, waits for them, and re-layouts: 33.5 us -> none  [the longest x6 15 us: mix_block(): jnp.einsum('in,hpn->ihp', c_proj.astype(jnp.float32), state_in, precision...]
    all_to_all x4 -> x0, starting transfers between devices: 29 us -> none  [sent_and_summed(): tiles = lax.all_to_all(split_up(array, dim, count), axis, 0, 0, tiled=True)]
  transfers between devices with their start and end apart: 18 -> 0, of which waited for: 6 -> 0; matrix products, arithmetic and copies ran while one was open for 50% -> 0% of each run, Pallas kernels for 0% -> 0%
where the time goes in v1:
time: 153 us; the launch traced here: 152 us
  Pallas kernels  146 us (95%)
  local copies, waits for them, and re-layouts  6.17 us (4%)
    pallas_call x1, Pallas kernels, per_device(): pl.pallas_call(kernel, out_shape=(shape((1, STEPS), f32), shape((8, WIDE)...  146 us
    unnamed x17, local copies, waits for them, and re-layouts  6.17 us

profile of v1, /device:TPU:1, one launch (start us, length us, event | category | flops | bytes accessed | tf_op | source)
XLA Modules:
  0.0 152.3 jit_solution(8174367794332149714)
XLA Ops:
  0.6 1.5 %copy.18 = f32[1,384,16]{2,1,0:T(8,128)} copy(f32[1,384,16]{1,2,0:T(8,128)} %param.15) | data formatting | bytes 49152 | tf_op args[3]
  2.2 145.5 %shard_map.163 = (f32[1,2]{1,0:T(1,128)}, f32[8,1024]{1,0:T(8,128)}, f32[1,16]{1,0:T(1,128)}, f32[1,16]{1,0:T(1,128)}, f32[1,16]{1,0:T(1,128)}, /*index=5*/f32[1,1024]{1,0:T(1,128)}) custom-call(bf16[384,1024]{1,0:T(8,128)(2,1)} %bitcast.15, bf16[384,1024]{1,0:T(8,128)(2,1)} %bitcast.16, bf16[384,256]{1,0:T(8,128)(2,1)} %bitcast.18, f32[384,16]{1,0:T(8,128)} %bitcast.14, ...), custom_call_target="tpu_custom_call" | custom-call | tf_op jit(solution)/shard_map/pallas_call | solution.py:553
  147.7 0.0 copy-start.4
  147.7 0.6 copy-done.4
  148.3 0.5 copy.25
  148.8 0.0 copy-start.3
  148.8 0.0 copy-start.2
  148.8 0.0 copy-start.1
  148.8 1.4 copy.26
  150.2 0.0 copy-done.3
  150.2 0.0 copy-start
  150.2 0.5 copy.27
  150.7 0.0 copy-done.2
  150.7 0.5 copy.28
  151.2 0.0 copy-done.1
  151.2 0.5 copy.29
  151.7 0.0 copy-done
  151.7 0.6 copy.30
Async XLA Ops:
  147.7 0.6 copy-start.4
  148.8 1.4 copy-start.3
  148.8 1.9 %copy-start.2 = (f32[1,16]{1,0:T(1,128)S(1)}, f32[1,16]{1,0:T(1,128)}, u32[]{:S(2)}) copy-start(f32[1,16]{1,0:T(1,128)} %get-tuple-element.15) | copy-start | bytes 196
  148.8 2.4 %copy-start.1 = (f32[1,16]{1,0:T(1,128)S(1)}, f32[1,16]{1,0:T(1,128)}, u32[]{:S(2)}) copy-start(f32[1,16]{1,0:T(1,128)} %get-tuple-element.16) | copy-start | bytes 196
  150.2 1.5 %copy-start = (f32[1,1024]{1,0:T(1,128)S(1)}, f32[1,1024]{1,0:T(1,128)}, u32[]{:S(2)}) copy-start(f32[1,1024]{1,0:T(1,128)} %get-tuple-element.17) | copy-start | bytes 12292

commit v2 on v1

--- a/solution.py
+++ b/solution.py
@@ -59,22 +59,67 @@
     return split[:, 0].reshape(count * 8, HALF), split[:, 1].reshape(count * 8, HALF)
 
 
-def kernel(
+INPUTS = (
+    "x_ref", "z_ref", "bc_ref", "raw_ref", "ids_ref", "cnt_ref", "tgt_ref", "w_ref", "dec_in", "bias_in",
+    "skip_in", "gain_in",
+)
+OUTPUTS = (
+    "loss_out", "w_out", "dec_out", "bias_out", "skip_out", "gain_out",
+)
+PARTS = "yxz"
+WIDTH = {"y": 256, "x": 128, "z": 128}
+FIRST = {"y": 0, "x": 256, "z": 384}
+
+
+def scratch():
+    dma, v = pltpu.SemaphoreType.DMA, pltpu.VMEM
+    rows_f, wide_f, wide_b = v((TOK, 128), f32), v((TOK, WIDE), f32), v((TOK, WIDE), bf16)
+    states, sixteen = v((CHUNKS + 1, STATE, WIDE), f32), v((N_SEQ, 16, HALF), bf16)
+    small, small16, small8 = v((16, 128), f32), v((N_SEQ, 16, 128), f32), v((N_DP, 16, 128), f32)
+    named = dict(
+        ex=v((128, WIDE), bf16), red=v((WIDE, 128), bf16), tri=v((CHUNK, CHUNK), f32), par=v((3, 8, 128), f32),
+        gain=v((1, WIDE), f32), wown=v((8, WIDE), f32), rawt=rows_f, wid=rows_f, dec_s=rows_f, ent=rows_f,
+        chain=v((CHUNKS, 8, WIDE), f32), fcol=v((CHUNKS, CHUNK, CHUNK), f32), sc=v((CHUNKS, CHUNK, CHUNK), f32),
+        xw=wide_b, wtd=wide_b, yin=wide_f, eexp=wide_f, gstate=v((CHUNKS, STATE, WIDE), f32), hst=states, apart=states,
+        normb=wide_b, ogb=wide_b, gb=wide_b, q2a=rows_f, ds1=rows_f, accs=v((2, 8, WIDE), f32),
+        hs=sixteen, hr=sixteen, hp=sixteen, hi=sixteen, gs=sixteen, gr=sixteen, gp=sixteen, gi=sixteen,
+        cs=v((8, 128), f32), cr=v((N_SEQ, 8, 128), f32), wfull=v((WIDE, WIDE), bf16),
+        wgp=v((N_Y, N_SEQ, 16, HALF), bf16), pr=v((N_Y, N_SEQ, 16, HALF), bf16),
+        sa=small, sar=small16, sb2=small, sbr=small8, t1=v((1, 128), f32), t1r=v((1, 128), f32), t2=v((1, 128), f32),
+        t2r=v((64, 1, 128), f32),
+    )
+    for p in PARTS:
+        w = WIDTH[p]
+        named["ag" + p] = v((128, 16, w), bf16)
+        named["sb" + p] = v((64, 16, w), bf16)
+        named["ra" + p] = v((3, N_SEQ, 16, w), bf16)
+        named["mid" + p] = v((N_SEQ, 16, w), bf16)
+        named["rb" + p] = v((N_SEQ, 16, w), bf16)
+    for name, count in dict(s_send=9, s_recv=9, s_ps=4, s_pr=4, g1s=3, g1r=3, g2s=3, g2r=3, g3s=3, g3r=3, r1s=3, r1r=3, r2s=3, r2r=3).items():
+        named[name] = dma((count,))
+    return named
+
+
+def kernel(*refs):
+    names = INPUTS + OUTPUTS + tuple(scratch())
+    assert len(names) == len(refs)
+    program(**dict(zip(names, refs)))
+
+
+def program(
     x_ref, z_ref, bc_ref, raw_ref, ids_ref, cnt_ref, tgt_ref, w_ref, dec_in, bias_in, skip_in, gain_in,
     loss_out, w_out, dec_out, bias_out, skip_out, gain_out,
-    ex, red, tri, par, gain, wown,
-    rawt, wid, dec_s, ent, tail, chain, fcol, sc,
-    xw, yin, eexp, silu, gstate, hst, apart, normb, ogb, gb, zin, ds1, accs,
-    hs, hr, hp, hi, gs, gr, gp, gi, cs, cr,
-    agb, wfull, wgp, pr, sb, rb,
-    sa, sar, sb2, sbr, ta, tar, tb, tbr,
-    s_send, s_recv, s_ag, s_agr, s_fs, s_fr, s_ps, s_pr, s_rs, s_rr,
+    ex, red, tri, par, gain, wown, rawt, wid, dec_s, ent, chain, fcol, sc,
+    xw, wtd, yin, eexp, gstate, hst, apart, normb, ogb, gb, q2a, ds1, accs,
+    hs, hr, hp, hi, gs, gr, gp, gi, cs, cr, wfull, wgp, pr, sa, sar, sb2, sbr, t1, t1r, t2, t2r,
+    s_send, s_recv, s_ps, s_pr, g1s, g1r, g2s, g2r, g3s, g3r, r1s, r1r, r2s, r2r, **part,
 ):
     dp, seq = lax.axis_index(DP), lax.axis_index(SEQ)
     yy, core = dp // 2, dp % 2
     partner = dp + 1 - 2 * core
     own_q = yy * N_SEQ + seq
-    own_b = dp * N_SEQ + seq
+    xx, zz = seq // 4, seq % 4
+    place = {"y": yy, "x": xx, "z": zz}
     MESH = pl.DeviceIdType.MESH
 
     def at(d, s):
@@ -110,6 +155,8 @@
     tri[...] = jnp.where(ti >= tj, 1.0, 0.0)
     rep = jnp.where(iota((HEADS, 128), 0) == (iota((HEADS, 128), 1) & 15), 1.0, 0.0)
 
+    spread = jnp.where((iota((128, 128), 0) & 15) == (iota((128, 128), 1) & 15), 1.0, 0.0)
+
     def tiled(ref):
         return jnp.dot(jnp.broadcast_to(ref[...], (8, HEADS)), rep, precision=highest, preferred_element_type=f32)
 
@@ -153,46 +200,94 @@
 
     lax.fori_loop(0, CHUNKS, prepare, 0)
 
+    def index_in(p, y, x, z):
+        return {"y": y * 16 + x * 4 + z, "x": x * 16 + y * 4 + z, "z": z * 16 + x * 4 + y}[p]
+
+    def plane_peer(p, k):
+        a, b = {"y": (xx, zz), "x": (yy, zz), "z": (xx, yy)}[p]
+        q = (a * 4 + b + k) % 16
+        if p == "y":
+            return dp, q, q
+        if p == "x":
+            return (q // 4) * 2 + core, xx * 4 + q % 4, q
+        return (q % 4) * 2 + core, (q // 4) * 4 + zz, q
+
+    def line_peer(p, k):
+        c = (place[p] + k) % 4
+        if p == "y":
+            return c * 2 + core, seq, c
+        if p == "x":
+            return dp, c * 4 + zz, c
+        return dp, xx * 4 + c, c
+
+    mine_in = {p: index_in(p, yy, xx, zz) for p in PARTS}
+
     def ag_start():
-        block = jnp.concatenate([wown[:, :HALF], wown[:, HALF:]], axis=0).astype(bf16)
-        agb[own_b] = block
-
-        def send(k, carry):
-            q = (own_q + k) % 64
-            remote(agb.at[own_b], agb.at[own_b], s_ag, s_agr.at[yy], (q // 16) * 2 + core, q % 16).start()
+        for n, p in enumerate(PARTS):
+            buf = part["ag" + p]
+            lanes = slice(FIRST[p], FIRST[p] + WIDTH[p])
+            right = slice(HALF + FIRST[p], HALF + FIRST[p] + WIDTH[p])
+            own = core * 64 + mine_in[p]
+            buf[own] = jnp.concatenate([wown[:, lanes], wown[:, right]], axis=0).astype(bf16)
+
+            def send(k, carry):
+                d, s, _ = plane_peer(p, k)
+                remote(buf.at[own], buf.at[own], g1s.at[n], g1r.at[n], d, s).start()
+                return carry
+
+            lax.fori_loop(1, 16, send, 0)
+
+    def ag_line():
+        for n, p in enumerate(PARTS):
+            buf = part["ag" + p]
+            piece = buf.at[pl.ds(0, 15)]
+            remote(piece, piece, g1s.at[n], g1r.at[n], partner, seq).wait_recv()
+            slab = buf.at[pl.ds(core * 64 + place[p] * 16, 16)]
+            for k in range(1, 4):
+                d, s, _ = line_peer(p, k)
+                remote(slab, slab, g2s.at[n], g2r.at[n], d, s).start()
+
+    def ag_cross():
+        for n, p in enumerate(PARTS):
+            buf = part["ag" + p]
+            piece = buf.at[pl.ds(0, 48)]
+            remote(piece, piece, g2s.at[n], g2r.at[n], partner, seq).wait_recv()
+            ours = buf.at[pl.ds(core * 64, 64)]
+            remote(ours, ours, g3s.at[n], g3r.at[n], partner, seq).start()
+
+    def ag_finish():
+        for n, p in enumerate(PARTS):
+            buf = part["ag" + p]
+            piece = buf.at[pl.ds((1 - core) * 64, 64)]
+            remote(piece, piece, g3s.at[n], g3r.at[n], partner, seq).wait_recv()
+
+        def unpack(d, carry):
+            base, y = (d % 2) * 64, d // 2
+            for p in PARTS:
+                buf, w = part["ag" + p], WIDTH[p]
+                if p == "y":
+                    blocks = [buf[pl.ds(base + y * 16, 16)].astype(f32)]
+                elif p == "x":
+                    blocks = [buf[pl.ds(base + x * 16 + y * 4, 4)].astype(f32) for x in range(4)]
+                else:
+                    blocks = [buf[pl.ds(base + z * 16 + x * 4 + y, 1)].astype(f32) for x in range(4) for z in range(4)]
+                tops, lows = [], []
+                for block in blocks:
+                    split = block.reshape(block.shape[0], 2, 8, w)
+                    tops.append(split[:, 0].reshape(-1, w))
+                    lows.append(split[:, 1].reshape(-1, w))
+                wfull[rows(d), FIRST[p] : FIRST[p] + w] = jnp.concatenate(tops, axis=0).astype(bf16)
+                wfull[rows(d), HALF + FIRST[p] : HALF + FIRST[p] + w] = jnp.concatenate(lows, axis=0).astype(bf16)
             return carry
 
-        lax.fori_loop(1, 64, send, 0)
-
-    def ag_finish():
-        copies = []
-        for k in range(N_Y):
-            y_k = (yy + k) % N_Y
-            first = (y_k * 2 + core) * N_SEQ
-            count = 15 if k == 0 else 16
-            piece = agb.at[pl.ds(first, count)]
-            remote(piece, piece, s_ag, s_agr.at[y_k], partner, seq).wait_recv()
-            whole = agb.at[pl.ds(first, N_SEQ)]
-            copy = remote(whole, whole, s_fs.at[k], s_fr.at[k], partner, seq)
-            copy.start()
-            copies.append(copy)
-        for k in range(N_Y):
-            y_k = (yy + k) % N_Y
-            other = (y_k * 2 + 1 - core) * N_SEQ
-            piece = agb.at[pl.ds(other, N_SEQ)]
-            remote(piece, piece, s_fs.at[k], s_fr.at[k], partner, seq).wait_recv()
-        sent = agb.at[pl.ds(0, 63)]
-        remote(sent, sent, s_ag, s_agr.at[0], partner, seq).wait_send()
-        for copy in copies:
-            copy.wait_send()
-
-        def unpack(d, carry):
-            left, right = rows_of(agb[pl.ds(d * N_SEQ, N_SEQ)].astype(f32))
-            wfull[rows(d), :HALF] = left.astype(bf16)
-            wfull[rows(d), HALF:] = right.astype(bf16)
-            return carry
-
         lax.fori_loop(0, N_DP, unpack, 0)
+
+    def ag_sent():
+        for n, p in enumerate(PARTS):
+            buf = part["ag" + p]
+            for count, ss, rs in ((15, g1s, g1r), (48, g2s, g2r), (64, g3s, g3r)):
+                piece = buf.at[pl.ds(0, count)]
+                remote(piece, piece, ss.at[n], rs.at[n], partner, seq).wait_send()
 
     def exchange_start(src, dst, n):
         def send(k, carry):
@@ -250,12 +345,10 @@
             through = jnp.exp(last) * jnp.where(seg_last == 0.0, 1.0, 0.0)
             wid[rows(c)] = width
             dec_s[rows(c)] = s
-            tail[rows(c)] = leaving
-            eexp[rows(c)] = expand(entering)
+            ent[rows(c)] = entering
             chain[c] = expand(jnp.broadcast_to(through, (8, 128)))
-            scaled = x_ref[rows(c)].astype(f32) * expand(width)
-            xw[rows(c)] = scaled.astype(bf16)
-            weighted = (scaled * expand(leaving)).astype(bf16)
+            weighted = (x_ref[rows(c)].astype(f32) * expand(width * leaving)).astype(bf16)
+            wtd[rows(c)] = weighted
             added = dot_tn(bc_ref[rows(c), :STATE], weighted)
             gstate[c] = added
             hst[0] = chain[c][0:1] * hst[0] + added
@@ -290,6 +383,8 @@
             s = dec_s[rows(c)]
             s_t = s.T
             scores = sc[c]
+            xw[rows(c)] = (x_ref[rows(c)].astype(f32) * expand(wid[rows(c)])).astype(bf16)
+            eexp[rows(c)] = expand(ent[rows(c)])
             for p in range(PAIRS):
                 parts = []
                 for h in (2 * p, 2 * p + 1):
@@ -301,6 +396,7 @@
             return carry
 
         lax.fori_loop(0, CHUNKS, inside, 0)
+        ag_line()
 
         half = seq % 2
 
@@ -322,6 +418,7 @@
         zeros4 = tuple(jnp.zeros((16, 128), f32) for _ in range(4))
         lax.fori_loop(0, N_SEQ, forward, zeros4)
         exchange_start(hp, hi, 2)
+        ag_cross()
         ag_finish()
         recv_wait(hi, 2, 15)
         for r in range(8):
@@ -359,7 +456,7 @@
             g_b = g.astype(bf16)
             gb[rows(c)] = g_b
             accs[1] += jnp.sum((g * x_f).reshape(16, 8, WIDE), axis=0)
-            ds1[rows(c)] = head_sum(g_b.astype(f32) * y_sum)
+            yin[rows(c)] = y_sum
             apart[c] = dot_tn(c_c, (g * eexp[rows(c)]).astype(bf16))
             hst[c + 1] = chain[c][0:1] * state + gstate[c]
             return loss
@@ -387,33 +484,49 @@
             remote(wgp.at[k], pr.at[k], s_ps.at[k], s_pr.at[k], partner, seq).start()
         for k in range(N_Y):
             y_k = (yy + k) % N_Y
-            d = y_k * 2 + core
-            mine = grad_rows(d)
+            mine = grad_rows(y_k * 2 + core)
             remote(wgp.at[k], pr.at[k], s_ps.at[k], s_pr.at[k], partner, seq).wait_recv()
-            sb[pl.ds(y_k * N_SEQ, N_SEQ)] = (mine + pr[k].astype(f32)).astype(bf16)
-
-            def send(j, carry):
-                s = (seq + j) % N_SEQ
-                remote(sb.at[y_k * N_SEQ + s], rb.at[own_q], s_rs, s_rr, d, s).start()
-                return carry
-
-            lax.fori_loop(1 if k == 0 else 0, N_SEQ, send, 0)
-        rb[own_q] = sb[own_q]
-
-        recv_wait(gr, 3, 15)
-
-        def backward(n, state):
-            i = N_SEQ - 1 - n
-            factors = carry_rows(i)
-            out = []
-            for m in range(4):
-                lanes = slice(128 * m, 128 * (m + 1))
-                gp[i, :, lanes] = state[m].astype(bf16)
-                out.append(factors[m] * state[m] + gr[i, :, lanes].astype(f32))
-            return tuple(out)
-
-        lax.fori_loop(0, N_SEQ, backward, zeros4)
-        exchange_start(gp, gi, 5)
+            both = (mine + pr[k].astype(f32)).astype(bf16)
+            part["sby"][pl.ds(y_k * 16, 16)] = both[:, :, : WIDTH["y"]]
+            if k > 0:
+                slab = part["sby"].at[pl.ds(y_k * 16, 16)]
+                remote(slab, part["ray"].at[k - 1], r1s.at[0], r1r.at[0], y_k * 2 + core, seq).start()
+            for p in "xz":
+                piece = both[:, :, FIRST[p] : FIRST[p] + WIDTH[p]]
+                for x in range(4):
+                    if p == "x":
+                        part["sbx"][pl.ds(x * 16 + y_k * 4, 4)] = piece[4 * x : 4 * x + 4]
+                    else:
+                        for z in range(4):
+                            part["sbz"][z * 16 + x * 4 + y_k] = piece[4 * x + z]
+        for n, p in ((1, "x"), (2, "z")):
+            for k in range(1, 4):
+                d, s, c = line_peer(p, k)
+                slab = part["sb" + p].at[pl.ds(c * 16, 16)]
+                remote(slab, part["ra" + p].at[k - 1], r1s.at[n], r1r.at[n], d, s).start()
+
+        def scatter_plane():
+            for n, p in enumerate(PARTS):
+                got, mid, dst = part["ra" + p], part["mid" + p], part["rb" + p]
+                remote(got, got, r1s.at[n], r1r.at[n], partner, seq).wait_recv()
+
+                def add(j, carry):
+                    value = part["sb" + p][place[p] * 16 + j].astype(f32)
+                    for k in range(3):
+                        value = value + got[k, j].astype(f32)
+                    mid[j] = value.astype(bf16)
+                    return carry
+
+                lax.fori_loop(0, 16, add, 0)
+                here = mine_in[p] % 16
+
+                def send(k, carry):
+                    d, s, q = plane_peer(p, k)
+                    remote(mid.at[q], dst.at[here], r2s.at[n], r2r.at[n], d, s).start()
+                    return carry
+
+                lax.fori_loop(1, 16, send, 0)
+                dst[here] = mid[here]
 
         def inside_back(c, carry):
             s = dec_s[rows(c)]
@@ -426,10 +539,30 @@
                     parts.append((jnp.exp(gap) * scores).astype(bf16))
                 mine = gb[rows(c), 128 * p : 128 * (p + 1)]
                 both = jnp.concatenate([mine * low_half, mine * high_half], axis=0)
-                zin[rows(c), 128 * p : 128 * (p + 1)] = dot(jnp.concatenate(parts, axis=1), both)
+                lanes = slice(128 * p, 128 * (p + 1))
+                eexp[rows(c), lanes] = dot(jnp.concatenate(parts, axis=1), both)
+            ds1[rows(c)] = head_sum(gb[rows(c)].astype(f32) * yin[rows(c)])
+            q2a[rows(c)] = head_sum(xw[rows(c)].astype(f32) * eexp[rows(c)])
             return carry
 
         lax.fori_loop(0, CHUNKS, inside_back, 0)
+
+        recv_wait(gr, 3, 15)
+
+        def backward(n, state):
+            i = N_SEQ - 1 - n
+            factors = carry_rows(i)
+            out = []
+            for m in range(4):
+                lanes = slice(128 * m, 128 * (m + 1))
+                gp[i, :, lanes] = state[m].astype(bf16)
+                out.append(factors[m] * state[m] + gr[i, :, lanes].astype(f32))
+            return tuple(out)
+
+        lax.fori_loop(0, N_SEQ, backward, zeros4)
+        exchange_start(gp, gi, 5)
+
+        scatter_plane()
 
         def summed(ref, count):
             value = ref[0]
@@ -446,14 +579,15 @@
             for h in range(2):
                 apart[3, 16 * r : 16 * r + 16, HALF * h : HALF * (h + 1)] = gi[2 * r + h].astype(f32)
 
-        def back(n, sums):
+        apart[2] = apart[2] + chain[2][0:1] * apart[3]
+        apart[1] = apart[1] + chain[1][0:1] * apart[2]
+
+        def back(c, sums):
             dec_g, bias_g = sums
-            c = CHUNKS - 1 - n
-            after = apart[3]
+            after = apart[c + 1]
             width = wid[rows(c)]
             z_t = dot(bc_ref[rows(c), :STATE], after.astype(bf16))
-            z_all = zin[rows(c)] + expand(tail[rows(c)]) * z_t
-            q2 = head_sum(xw[rows(c)].astype(f32) * z_all)
+            q2 = q2a[rows(c)] + head_sum(wtd[rows(c)].astype(f32) * z_t)
             ends = jnp.sum((after * hst[c + 1]).reshape(16, 8, WIDE), axis=0)
             end_h = jnp.sum(head_sum(ends), axis=0, keepdims=True)
             d_s = ds1[rows(c)] - q2
@@ -465,7 +599,6 @@
             sig = 1.0 / (1.0 + jnp.exp(-pre))
             dec_g = dec_g - jnp.sum(d_a * (rate * width), axis=0, keepdims=True)
             bias_g = bias_g + jnp.sum(d_w * sig, axis=0, keepdims=True)
-            apart[3] = apart[c] + chain[c][0:1] * after
             return dec_g, bias_g
 
         zero_row = jnp.zeros((1, 128), f32)
@@ -474,25 +607,40 @@
         recv_wait(sbr, 6, 7)
         sums_a = summed(sbr, N_DP)
 
-        got = rb.at[pl.ds(0, 63)]
-        remote(got, got, s_rs, s_rr, partner, seq).wait_recv()
-
-        def add_up(q, value):
-            return value + rb[q].astype(f32)
-
-        grad = lax.fori_loop(0, 64, add_up, jnp.zeros((16, HALF), f32))
-        square = jnp.sum(jnp.sum(grad * grad, axis=1, keepdims=True), axis=0, keepdims=True)
-        ta[...] = jnp.where(
-            sub == 0, dec_g, jnp.where(sub == 1, bias_g, jnp.where(sub == 2, jnp.broadcast_to(square, (8, 128)), 0.0))
-        )
-        spread_start(ta, tar, 7)
-        recv_wait(tar, 7, 15)
-        tb[...] = summed(tar, N_SEQ)
-        cross_start(tb, tbr, 8)
-        recv_wait(tbr, 8, 7)
-        sums_b = summed(tbr, N_DP)
-
-        dec_g, bias_g, squares = sums_b[0:1], sums_b[1:2], sums_b[2:3]
+        ag_sent()
+
+        grad, square = {}, jnp.zeros((1, 1), f32)
+        for n, p in enumerate(PARTS):
+            dst = part["rb" + p]
+            got = dst.at[pl.ds(0, 15)]
+            remote(got, got, r2s.at[n], r2r.at[n], partner, seq).wait_recv()
+            value = dst[0].astype(f32)
+            for q in range(1, 16):
+                value = value + dst[q].astype(f32)
+            grad[p] = value
+            square = square + jnp.sum(jnp.sum(value * value, axis=1, keepdims=True), axis=0, keepdims=True)
+        t1[...] = jnp.where(lane < 16, dec_g, jnp.where(lane < 32, bias_g, jnp.where(lane == 32, square, 0.0)))
+        pair = remote(t1, t1r, s_send.at[7], s_recv.at[7], partner, seq)
+        pair.start()
+        pair.wait_recv()
+        t2[...] = t1[...] + t1r[...]
+
+        def send_small(k, carry):
+            q = (own_q + k) % 64
+            remote(t2, t2r.at[own_q], s_send.at[8], s_recv.at[8], (q // 16) * 2 + core, q % 16).start()
+            return carry
+
+        lax.fori_loop(1, 64, send_small, 0)
+        t2r[own_q] = t2[...]
+        recv_wait(t2r, 8, 63)
+        sums_b = jnp.sum(t2r[...], axis=0)
+
+        def heads_at(first):
+            picked = jnp.where((lane >= first) & (lane < first + 16), sums_b, 0.0)
+            return jnp.dot(jnp.broadcast_to(picked, (8, 128)), spread, precision=highest, preferred_element_type=f32)[0:1]
+
+        dec_g, bias_g = heads_at(0), heads_at(16)
+        squares = jnp.sum(jnp.where(lane == 32, sums_b, 0.0), axis=1, keepdims=True)
         gain_rows, skip_g, loss_all = sums_a[0:8], sums_a[8:9], sums_a[9:10]
         small = jnp.sum(
             jnp.where(lane < HEADS, dec_g * dec_g + bias_g * bias_g + skip_g * skip_g, 0.0), axis=1, keepdims=True
@@ -506,9 +654,10 @@
         for r in range(8):
             lanes = slice(128 * r, 128 * (r + 1))
             gain[:, lanes] = gain[:, lanes] - move * gain_rows[r : r + 1]
-        move_w = jnp.broadcast_to(move[:, 0:1], (8, HALF))
-        wown[:, :HALF] = wown[:, :HALF] - move_w * grad[0:8]
-        wown[:, HALF:] = wown[:, HALF:] - move_w * grad[8:16]
+        for p in PARTS:
+            for h in range(2):
+                lanes = slice(HALF * h + FIRST[p], HALF * h + FIRST[p] + WIDTH[p])
+                wown[:, lanes] = wown[:, lanes] - move * grad[p][8 * h : 8 * h + 8]
 
         send_wait(hr, 0, 15)
         send_wait(cr, 1, 15)
@@ -517,11 +666,14 @@
         send_wait(sar, 4, 15)
         send_wait(gi, 5, 15)
         send_wait(sbr, 6, 7)
-        send_wait(tar, 7, 15)
-        send_wait(tbr, 8, 7)
+        pair.wait_send()
+        send_wait(t2r, 8, 63)
         for k in range(N_Y):
             remote(wgp.at[k], pr.at[k], s_ps.at[k], s_pr.at[k], partner, seq).wait_send()
-        remote(got, got, s_rs, s_rr, partner, seq).wait_send()
+        for n, p in enumerate(PARTS):
+            got, dst = part["ra" + p], part["rb" + p].at[pl.ds(0, 15)]
+            remote(got, got, r1s.at[n], r1r.at[n], partner, seq).wait_send()
+            remote(dst, dst, r2s.at[n], r2r.at[n], partner, seq).wait_send()
 
         @pl.when(step == 0)
         def _():
@@ -542,14 +694,7 @@
 def per_device(x, z, bc, raw, ids, counts, target, weight, dec, bias, skip, gain):
     vmem = pl.BlockSpec(memory_space=pltpu.VMEM)
     smem = pl.BlockSpec(memory_space=pltpu.SMEM)
-    dma = pltpu.SemaphoreType.DMA
     shape = jax.ShapeDtypeStruct
-    v = pltpu.VMEM
-    rows_f = v((TOK, 128), f32)
-    wide_f = v((TOK, WIDE), f32)
-    wide_b = v((TOK, WIDE), bf16)
-    states = v((CHUNKS + 1, STATE, WIDE), f32)
-    sixteen = v((N_SEQ, 16, HALF), bf16)
     outs = pl.pallas_call(
         kernel,
         out_shape=(
@@ -558,21 +703,7 @@
         ),
         in_specs=[vmem] * 5 + [smem] + [vmem] * 6,
         out_specs=(vmem,) * 6,
-        scratch_shapes=[
-            v((128, WIDE), bf16), v((WIDE, 128), bf16), v((CHUNK, CHUNK), f32), v((3, 8, 128), f32), v((1, WIDE), f32),
-            v((8, WIDE), f32),
-            rows_f, rows_f, rows_f, v((8, 128), f32), rows_f, v((CHUNKS, 8, WIDE), f32),
-            v((CHUNKS, CHUNK, CHUNK), f32), v((CHUNKS, CHUNK, CHUNK), f32),
-            wide_b, wide_f, wide_f, v((8, 128), f32), v((CHUNKS, STATE, WIDE), f32), states, states, wide_b, wide_b, wide_b,
-            wide_f, rows_f, v((2, 8, WIDE), f32),
-            sixteen, sixteen, sixteen, sixteen, sixteen, sixteen, sixteen, sixteen, v((8, 128), f32),
-            v((N_SEQ, 8, 128), f32),
-            v((128, 16, HALF), bf16), v((WIDE, WIDE), bf16), v((N_Y, N_SEQ, 16, HALF), bf16),
-            v((N_Y, N_SEQ, 16, HALF), bf16), v((64, 16, HALF), bf16), v((64, 16, HALF), bf16),
-            v((16, 128), f32), v((N_SEQ, 16, 128), f32), v((16, 128), f32), v((N_DP, 16, 128), f32),
-            v((8, 128), f32), v((N_SEQ, 8, 128), f32), v((8, 128), f32), v((N_DP, 8, 128), f32),
-            dma((9,)), dma((9,)), dma, dma((N_Y,)), dma((N_Y,)), dma((N_Y,)), dma((N_Y,)), dma((N_Y,)), dma, dma,
-        ],
+        scratch_shapes=list(scratch().values()),
         compiler_params=pltpu.CompilerParams(
             collective_id=0, has_side_effects=True, vmem_limit_bytes=62 * 1024 * 1024
         ),

time: 153 us -> 117 us (0.76)
  Pallas kernels: 146 us -> 110 us
    pallas_call x1, Pallas kernels: 146 us -> 110 us  [per_device(): pl.pallas_call(kernel, out_shape=(shape((1, STEPS), f32), shape((8, WIDE)...]
where the time goes in v2:
time: 117 us
  Pallas kernels  110 us (94%)
  local copies, waits for them, and re-layouts  6.17 us (5%)
    pallas_call x1, Pallas kernels, per_device(): pl.pallas_call(kernel, out_shape=(shape((1, STEPS), f32), shape((8, WIDE)...  110 us
    unnamed x17, local copies, waits for them, and re-layouts  6.17 us

profile of v2, /device:TPU:1, one launch (start us, length us, event | category | flops | bytes accessed | tf_op | source)
XLA Modules:
  0.0 117.1 jit_solution(10476075596664756913)
XLA Ops:
  0.6 1.5 %copy.18 = f32[1,384,16]{2,1,0:T(8,128)} copy(f32[1,384,16]{1,2,0:T(8,128)} %param.15) | data formatting | bytes 49152 | tf_op args[3]
  2.2 110.2 %shard_map.163 = (f32[1,2]{1,0:T(1,128)}, f32[8,1024]{1,0:T(8,128)}, f32[1,16]{1,0:T(1,128)}, f32[1,16]{1,0:T(1,128)}, f32[1,16]{1,0:T(1,128)}, /*index=5*/f32[1,1024]{1,0:T(1,128)}) custom-call(bf16[384,1024]{1,0:T(8,128)(2,1)} %bitcast.15, bf16[384,1024]{1,0:T(8,128)(2,1)} %bitcast.16, bf16[384,256]{1,0:T(8,128)(2,1)} %bitcast.18, f32[384,16]{1,0:T(8,128)} %bitcast.14, ...), custom_call_target="tpu_custom_call" | custom-call | tf_op jit(solution)/shard_map/pallas_call | solution.py:698
  112.4 0.0 copy-start.4
  112.4 0.6 copy-done.4
  113.0 0.5 copy.25
  113.5 0.0 copy-start.3
  113.5 0.0 copy-start.2
  113.5 0.0 copy-start.1
  113.5 1.4 %copy.26 = f32[8,1024]{1,0:T(8,128)} copy(f32[8,1024]{1,0:T(8,128)} %get-tuple-element.25) | data formatting | bytes 65536
  114.9 0.0 copy-done.3
  114.9 0.0 copy-start
  114.9 0.5 copy.27
  115.4 0.0 copy-done.2
  115.4 0.5 copy.28
  116.0 0.0 copy-done.1
  116.0 0.5 copy.29
  116.5 0.0 copy-done
  116.5 0.6 copy.30
Async XLA Ops:
  112.4 0.6 copy-start.4
  113.5 1.4 %copy-start.3 = (f32[1,16]{1,0:T(1,128)S(1)}, f32[1,16]{1,0:T(1,128)}, u32[]{:S(2)}) copy-start(f32[1,16]{1,0:T(1,128)} %get-tuple-element.14) | copy-start | bytes 196
  113.5 1.9 %copy-start.2 = (f32[1,16]{1,0:T(1,128)S(1)}, f32[1,16]{1,0:T(1,128)}, u32[]{:S(2)}) copy-start(f32[1,16]{1,0:T(1,128)} %get-tuple-element.15) | copy-start | bytes 196
  113.5 2.4 %copy-start.1 = (f32[1,16]{1,0:T(1,128)S(1)}, f32[1,16]{1,0:T(1,128)}, u32[]{:S(2)}) copy-start(f32[1,16]{1,0:T(1,128)} %get-tuple-element.16) | copy-start | bytes 196
  114.9 1.5 %copy-start = (f32[1,1024]{1,0:T(1,128)S(1)}, f32[1,1024]{1,0:T(1,128)}, u32[]{:S(2)}) copy-start(f32[1,1024]{1,0:T(1,128)} %get-tuple-element.17) | copy-start | bytes 12292

commit v3 on v2

--- a/solution.py
+++ b/solution.py
@@ -60,12 +60,9 @@
 
 
 INPUTS = (
-    "x_ref", "z_ref", "bc_ref", "raw_ref", "ids_ref", "cnt_ref", "tgt_ref", "w_ref", "dec_in", "bias_in",
-    "skip_in", "gain_in",
+    "x_in", "z_in", "bc_in", "raw_in", "ids_ref", "cnt_ref", "tgt_in", "w_ref", "dec_in", "bias_in", "skip_in", "gain_in",
 )
-OUTPUTS = (
-    "loss_out", "w_out", "dec_out", "bias_out", "skip_out", "gain_out",
-)
+OUTPUTS = ("packed_out",)
 PARTS = "yxz"
 WIDTH = {"y": 256, "x": 128, "z": 128}
 FIRST = {"y": 0, "x": 256, "z": 384}
@@ -77,9 +74,11 @@
     states, sixteen = v((CHUNKS + 1, STATE, WIDE), f32), v((N_SEQ, 16, HALF), bf16)
     small, small16, small8 = v((16, 128), f32), v((N_SEQ, 16, 128), f32), v((N_DP, 16, 128), f32)
     named = dict(
+        x_ref=wide_b, z_ref=wide_b, bc_ref=v((TOK, 2 * STATE), bf16), tgt_ref=wide_b, s_in=dma((4,)),
+        act=wide_f, gat=wide_f, dnf=wide_f, invs=rows_f,
         ex=v((128, WIDE), bf16), red=v((WIDE, 128), bf16), tri=v((CHUNK, CHUNK), f32), par=v((3, 8, 128), f32),
         gain=v((1, WIDE), f32), wown=v((8, WIDE), f32), rawt=rows_f, wid=rows_f, dec_s=rows_f, ent=rows_f,
-        chain=v((CHUNKS, 8, WIDE), f32), fcol=v((CHUNKS, CHUNK, CHUNK), f32), sc=v((CHUNKS, CHUNK, CHUNK), f32),
+        chain=v((8, WIDE), f32), fcol=v((CHUNKS, CHUNK, CHUNK), f32), sc=v((CHUNKS, CHUNK, CHUNK), f32),
         xw=wide_b, wtd=wide_b, yin=wide_f, eexp=wide_f, gstate=v((CHUNKS, STATE, WIDE), f32), hst=states, apart=states,
         normb=wide_b, ogb=wide_b, gb=wide_b, q2a=rows_f, ds1=rows_f, accs=v((2, 8, WIDE), f32),
         hs=sixteen, hr=sixteen, hp=sixteen, hi=sixteen, gs=sixteen, gr=sixteen, gp=sixteen, gi=sixteen,
@@ -107,8 +106,8 @@
 
 
 def program(
-    x_ref, z_ref, bc_ref, raw_ref, ids_ref, cnt_ref, tgt_ref, w_ref, dec_in, bias_in, skip_in, gain_in,
-    loss_out, w_out, dec_out, bias_out, skip_out, gain_out,
+    x_in, z_in, bc_in, raw_in, ids_ref, cnt_ref, tgt_in, w_ref, dec_in, bias_in, skip_in, gain_in,
+    packed_out, x_ref, z_ref, bc_ref, tgt_ref, s_in, act, gat, dnf, invs,
     ex, red, tri, par, gain, wown, rawt, wid, dec_s, ent, chain, fcol, sc,
     xw, wtd, yin, eexp, gstate, hst, apart, normb, ogb, gb, q2a, ds1, accs,
     hs, hr, hp, hi, gs, gr, gp, gi, cs, cr, wfull, wgp, pr, sa, sar, sb2, sbr, t1, t1r, t2, t2r,
@@ -132,18 +131,24 @@
 
     barrier = pltpu.get_barrier_semaphore()
 
-    def greet_same(k, carry):
-        q = (own_q + k) % 64
-        pl.semaphore_signal(barrier, 1, device_id=at((q // 16) * 2 + core, q % 16), device_id_type=MESH)
-        return carry
-
-    lax.fori_loop(1, 64, greet_same, 0)
-
-    def greet_other(k, carry):
-        pl.semaphore_signal(barrier, 1, device_id=at(k * 2 + 1 - core, seq), device_id_type=MESH)
-        return carry
-
-    lax.fori_loop(0, N_Y, greet_other, 0)
+    dps = [((yy + k) % 4) * 2 + core for k in range(4)]
+    seqs = {(a, b): ((xx + a) % 4) * 4 + (zz + b) % 4 for a in range(4) for b in range(4)}
+
+    def hops(offset):
+        return sum(min(k, 4 - k) for k in offset)
+
+    chips = [(a, b, c) for a in range(4) for b in range(4) for c in range(4)]
+    far_first = sorted(chips[1:], key=lambda offset: -hops(offset))
+    for a, b, c in far_first:
+        pl.semaphore_signal(barrier, 1, device_id=at(dps[a], seqs[b, c]), device_id_type=MESH)
+    for k in range(4):
+        pl.semaphore_signal(barrier, 1, device_id=at(dps[k] + 1 - 2 * core, seq), device_id_type=MESH)
+    loads = [
+        pltpu.make_async_copy(source, target, s_in.at[n])
+        for n, (source, target) in enumerate(((bc_in, bc_ref), (x_in, x_ref), (z_in, z_ref), (tgt_in, tgt_ref)))
+    ]
+    for load in loads:
+        load.start()
 
     row = iota((CHUNK, WIDE), 0)
     col = iota((CHUNK, WIDE), 1)
@@ -165,7 +170,10 @@
     par[2] = tiled(skip_in)
     gain[...] = gain_in[...]
     wown[...] = w_ref[...]
-    rawt[...] = jnp.dot(raw_ref[...], rep, precision=highest, preferred_element_type=f32)
+    rawt[...] = lax.dot_general(
+        raw_in[...], rep, (((0,), (0,)), ((), ())), precision=highest, preferred_element_type=f32
+    )
+    loads[0].wait()
 
     def expand(v):
         return dot(three_parts(v), ex[...])
@@ -199,6 +207,7 @@
         return carry
 
     lax.fori_loop(0, CHUNKS, prepare, 0)
+    loads[1].wait()
 
     def index_in(p, y, x, z):
         return {"y": y * 16 + x * 4 + z, "x": x * 16 + y * 4 + z, "z": z * 16 + x * 4 + y}[p]
@@ -256,13 +265,8 @@
             remote(ours, ours, g3s.at[n], g3r.at[n], partner, seq).start()
 
     def ag_finish():
-        for n, p in enumerate(PARTS):
-            buf = part["ag" + p]
-            piece = buf.at[pl.ds((1 - core) * 64, 64)]
-            remote(piece, piece, g3s.at[n], g3r.at[n], partner, seq).wait_recv()
-
-        def unpack(d, carry):
-            base, y = (d % 2) * 64, d // 2
+        def unpack(y, its_core):
+            base, d = its_core * 64, y * 2 + its_core
             for p in PARTS:
                 buf, w = part["ag" + p], WIDTH[p]
                 if p == "y":
@@ -278,9 +282,14 @@
                     lows.append(split[:, 1].reshape(-1, w))
                 wfull[rows(d), FIRST[p] : FIRST[p] + w] = jnp.concatenate(tops, axis=0).astype(bf16)
                 wfull[rows(d), HALF + FIRST[p] : HALF + FIRST[p] + w] = jnp.concatenate(lows, axis=0).astype(bf16)
-            return carry
-
-        lax.fori_loop(0, N_DP, unpack, 0)
+            return its_core
+
+        lax.fori_loop(0, N_Y, unpack, core)
+        for n, p in enumerate(PARTS):
+            buf = part["ag" + p]
+            piece = buf.at[pl.ds((1 - core) * 64, 64)]
+            remote(piece, piece, g3s.at[n], g3r.at[n], partner, seq).wait_recv()
+        lax.fori_loop(0, N_Y, unpack, 1 - core)
 
     def ag_sent():
         for n, p in enumerate(PARTS):
@@ -328,38 +337,37 @@
         dec_t, bias_t, skip_t = par[0, 0:1], par[1, 0:1], par[2, 0:1]
         rate = jnp.exp(dec_t)
 
-        hst[0] = jnp.zeros((STATE, WIDE), f32)
-
-        def begin(c, carried):
+        pre = rawt[...] + bias_t
+        u = jnp.exp(-jnp.abs(pre))
+        v = 1.0 + u
+        log1p = jnp.where(v == 1.0, u, jnp.log(v) * u / jnp.where(v == 1.0, 1.0, v - 1.0))
+        widths = jnp.maximum(pre, 0.0) + log1p
+        wid[...] = widths
+        sub8, lane8 = iota((8, 128), 0), iota((8, 128), 1)
+        through = jnp.zeros((8, 128), f32)
+        carried = jnp.ones((1, 128), f32)
+        for c in range(CHUNKS):
+            span = slice(c * CHUNK, (c + 1) * CHUNK)
             seg = fcol[c]
-            pre = rawt[rows(c)] + bias_t
-            u = jnp.exp(-jnp.abs(pre))
-            v = 1.0 + u
-            log1p = jnp.where(v == 1.0, u, jnp.log(v) * u / jnp.where(v == 1.0, 1.0, v - 1.0))
-            width = jnp.maximum(pre, 0.0) + log1p
+            width = widths[span]
             s = jnp.dot(tri[...], -rate * width, precision=highest, preferred_element_type=f32)
             last = s[CHUNK - 1 : CHUNK]
             seg_last = seg[CHUNK - 1 : CHUNK]
-            entering = jnp.exp(s) * jnp.where(seg == 0.0, 1.0, 0.0)
             leaving = jnp.exp(last - s) * jnp.where(seg == seg_last, 1.0, 0.0)
-            through = jnp.exp(last) * jnp.where(seg_last == 0.0, 1.0, 0.0)
-            wid[rows(c)] = width
-            dec_s[rows(c)] = s
-            ent[rows(c)] = entering
-            chain[c] = expand(jnp.broadcast_to(through, (8, 128)))
-            weighted = (x_ref[rows(c)].astype(f32) * expand(width * leaving)).astype(bf16)
-            wtd[rows(c)] = weighted
-            added = dot_tn(bc_ref[rows(c), :STATE], weighted)
-            gstate[c] = added
-            hst[0] = chain[c][0:1] * hst[0] + added
-            return carried * through
-
-        carried = lax.fori_loop(0, CHUNKS, begin, jnp.ones((1, 128), f32))
+            passing = jnp.exp(last) * jnp.where(seg_last == 0.0, 1.0, 0.0)
+            dec_s[span] = s
+            ent[span] = jnp.exp(s) * jnp.where(seg == 0.0, 1.0, 0.0)
+            weighted = (x_ref[span].astype(f32) * expand(width * leaving)).astype(bf16)
+            wtd[span] = weighted
+            gstate[c] = dot_tn(bc_ref[span, :STATE], weighted)
+            through = jnp.where(sub8 == c, passing, through)
+            carried = carried * passing
+        chain[...] = expand(through)
         wide8 = jnp.broadcast_to(carried, (8, 128))
-        sub8, lane8 = iota((8, 128), 0), iota((8, 128), 1)
         even = jnp.sum(jnp.where(lane8 == 2 * sub8, wide8, 0.0), axis=1, keepdims=True)
         odd = jnp.sum(jnp.where(lane8 == 2 * sub8 + 1, wide8, 0.0), axis=1, keepdims=True)
         cs[...] = jnp.where(lane8 < HEAD, even, odd)
+        hst[0] = gstate[2] + chain[2:3] * (gstate[1] + chain[1:2] * gstate[0])
 
         def to_blocks(state, out):
             for r in range(8):
@@ -370,14 +378,20 @@
 
         @pl.when(step == 0)
         def _():
+            loads[2].wait()
+
+            def activate(c, carry):
+                z_f = z_ref[rows(c)].astype(f32)
+                act[rows(c)] = z_f / (1.0 + jnp.exp(-z_f))
+                return carry
+
+            lax.fori_loop(0, CHUNKS, activate, 0)
+            loads[3].wait()
             pl.semaphore_wait(barrier, 67)
+            ag_start()
 
         exchange_start(hs, hr, 0)
         spread_start(cs, cr, 1)
-
-        @pl.when(step == 0)
-        def _():
-            ag_start()
 
         def inside(c, carry):
             s = dec_s[rows(c)]
@@ -428,43 +442,58 @@
         skip_e = expand(jnp.broadcast_to(skip_t, (8, 128)))[0:1]
         gain_e = gain[...]
         scale = 2.0 / (WIDE * total_f)
-        accs[...] = jnp.zeros(accs.shape, f32)
-
-        def mix(c, loss):
+        accs[1] = jnp.zeros((8, WIDE), f32)
+
+        for c in range(CHUNKS):
+            span = slice(c * CHUNK, (c + 1) * CHUNK)
             state = hst[c]
-            b_c, c_c = bc_ref[rows(c), :STATE], bc_ref[rows(c), STATE:]
-            y_sum = yin[rows(c)] + eexp[rows(c)] * dot(c_c, state.astype(bf16))
-            x_f = x_ref[rows(c)].astype(f32)
-            z_f = z_ref[rows(c)].astype(f32)
-            act = z_f / (1.0 + jnp.exp(-z_f))
-            gated = (y_sum + skip_e * x_f) * act
+            y_sum = yin[span] + eexp[span] * dot(bc_ref[span, STATE:], state.astype(bf16))
+            yin[span] = y_sum
+            gated = (y_sum + skip_e * x_ref[span].astype(f32)) * act[span]
+            gat[span] = gated
             inv = lax.rsqrt(jnp.sum(gated * gated, axis=1, keepdims=True) * (1.0 / WIDE) + norm_floor)
-            normed = (gated * gain_e * inv).astype(bf16)
-            normb[rows(c)] = normed
-            res = dot(normed, wfull[...]) - tgt_ref[rows(c)].astype(f32)
-            position = seq * TOK + c * CHUNK + iota((CHUNK, 1), 0)
-            scored = jnp.where(position < own_count, 1.0, 0.0)
-            loss = loss + jnp.sum(jnp.sum(res * res, axis=1, keepdims=True) * scored, axis=0, keepdims=True)
-            og = (res * (scored * scale)).astype(bf16)
-            ogb[rows(c)] = og
-            d_norm = dot_nt(og, wfull[...])
-            d_gr = d_norm * gated * inv
-            accs[0] += jnp.sum(d_gr.reshape(16, 8, WIDE), axis=0)
-            inner = jnp.sum(d_gr * gain_e, axis=1, keepdims=True) * (1.0 / WIDE)
-            d_gated = inv * (gain_e * d_norm - gated * (inv * inner))
-            g = d_gated * act
-            g_b = g.astype(bf16)
-            gb[rows(c)] = g_b
-            accs[1] += jnp.sum((g * x_f).reshape(16, 8, WIDE), axis=0)
-            yin[rows(c)] = y_sum
-            apart[c] = dot_tn(c_c, (g * eexp[rows(c)]).astype(bf16))
-            hst[c + 1] = chain[c][0:1] * state + gstate[c]
-            return loss
-
-        loss = lax.fori_loop(0, CHUNKS, mix, jnp.zeros((1, 1), f32))
-        entry = apart[0] + chain[0][0:1] * (apart[1] + chain[1][0:1] * apart[2])
+            invs[span] = jnp.broadcast_to(inv, (CHUNK, 128))
+            normb[span] = (gated * gain_e * inv).astype(bf16)
+            hst[c + 1] = chain[c : c + 1] * state + gstate[c]
+        position = seq * TOK + iota((TOK, 256), 0)
+        scored = jnp.where(position < own_count, 1.0, 0.0)
+        losses_8 = jnp.zeros((8, 256), f32)
+        for n in range(4):
+            lanes = slice(256 * n, 256 * (n + 1))
+            res = (dot(normb[...], wfull[:, lanes]) - tgt_ref[:, lanes].astype(f32)) * scored
+            losses_8 = losses_8 + jnp.sum((res * res).reshape(TOK // 8, 8, 256), axis=0)
+            ogb[:, lanes] = (res * scale).astype(bf16)
+        loss = jnp.sum(jnp.sum(losses_8, axis=1, keepdims=True), axis=0, keepdims=True)
+        inner_l = jnp.zeros((TOK, 128), f32)
+        for n in range(4):
+            lanes = slice(256 * n, 256 * (n + 1))
+            d_norm = dot_nt(ogb[...], wfull[lanes, :])
+            dnf[:, lanes] = d_norm
+            inv_2 = jnp.concatenate([invs[...], invs[...]], axis=1)
+            d_gr = d_norm * gat[:, lanes] * inv_2
+            accs[0, :, lanes] = jnp.sum(d_gr.reshape(TOK // 8, 8, 256), axis=0)
+            term = d_gr * gain_e[:, lanes]
+            inner_l = inner_l + (term[:, :128] + term[:, 128:])
+        inner = jnp.sum(inner_l, axis=1, keepdims=True) * (1.0 / WIDE)
+        for c in range(CHUNKS):
+            span = slice(c * CHUNK, (c + 1) * CHUNK)
+            inv = invs[span, 0:1]
+            g = inv * (gain_e * dnf[span] - gat[span] * (inv * inner[span])) * act[span]
+            gb[span] = g.astype(bf16)
+            accs[1] += jnp.sum((g * x_ref[span].astype(f32)).reshape(16, 8, WIDE), axis=0)
+            apart[c] = dot_tn(bc_ref[span, STATE:], (g * eexp[span]).astype(bf16))
+        entry = apart[0] + chain[0:1] * (apart[1] + chain[1:2] * apart[2])
         to_blocks(entry, gs)
         exchange_start(gs, gr, 3)
+        def grad_rows(d):
+            lanes = pl.ds(pl.multiple_of(d * 128, 128), 128)
+            return blocks_of(dot_tn(normb[:, lanes], ogb[...]))
+
+        for k in (1, 2, 3, 0):
+            y_k = (yy + k) % N_Y
+            d = y_k * 2 + 1 - core
+            wgp[k] = grad_rows(d).astype(bf16)
+            remote(wgp.at[k], pr.at[k], s_ps.at[k], s_pr.at[k], partner, seq).start()
         gain_g = jnp.sum(accs[0], axis=0, keepdims=True)
         for r in range(8):
             sa[r : r + 1, :] = gain_g[:, 128 * r : 128 * (r + 1)]
@@ -473,16 +502,7 @@
         sa[8:16, :] = jnp.where(sub == 0, skip_g, jnp.where(sub == 1, jnp.broadcast_to(loss, (8, 128)), 0.0))
         spread_start(sa, sar, 4)
 
-        def grad_rows(d):
-            lanes = pl.ds(pl.multiple_of(d * 128, 128), 128)
-            return blocks_of(dot_tn(normb[:, lanes], ogb[...]))
-
-        for k in range(N_Y):
-            y_k = (yy + k) % N_Y
-            d = y_k * 2 + 1 - core
-            wgp[k] = grad_rows(d).astype(bf16)
-            remote(wgp.at[k], pr.at[k], s_ps.at[k], s_pr.at[k], partner, seq).start()
-        for k in range(N_Y):
+        for k in (1, 2, 3, 0):
             y_k = (yy + k) % N_Y
             mine = grad_rows(y_k * 2 + core)
             remote(wgp.at[k], pr.at[k], s_ps.at[k], s_pr.at[k], partner, seq).wait_recv()
@@ -579,8 +599,8 @@
             for h in range(2):
                 apart[3, 16 * r : 16 * r + 16, HALF * h : HALF * (h + 1)] = gi[2 * r + h].astype(f32)
 
-        apart[2] = apart[2] + chain[2][0:1] * apart[3]
-        apart[1] = apart[1] + chain[1][0:1] * apart[2]
+        apart[2] = apart[2] + chain[2:3] * apart[3]
+        apart[1] = apart[1] + chain[1:2] * apart[2]
 
         def back(c, sums):
             dec_g, bias_g = sums
@@ -625,12 +645,8 @@
         pair.wait_recv()
         t2[...] = t1[...] + t1r[...]
 
-        def send_small(k, carry):
-            q = (own_q + k) % 64
-            remote(t2, t2r.at[own_q], s_send.at[8], s_recv.at[8], (q // 16) * 2 + core, q % 16).start()
-            return carry
-
-        lax.fori_loop(1, 64, send_small, 0)
+        for a, b, c in far_first:
+            remote(t2, t2r.at[own_q], s_send.at[8], s_recv.at[8], dps[a], seqs[b, c]).start()
         t2r[own_q] = t2[...]
         recv_wait(t2r, 8, 63)
         sums_b = jnp.sum(t2r[...], axis=0)
@@ -683,35 +699,50 @@
         return jnp.where(iota((1, STEPS), 1) == step, step_loss, losses)
 
     losses = lax.fori_loop(0, STEPS, one_step, jnp.zeros((1, STEPS), f32))
-    loss_out[...] = losses
-    w_out[...] = wown[...]
-    dec_out[...] = par[0, 0:1, :HEADS]
-    bias_out[...] = par[1, 0:1, :HEADS]
-    skip_out[...] = par[2, 0:1, :HEADS]
-    gain_out[...] = gain[...]
+    packed_out[0:8] = wown[...]
+    packed_out[8:9] = gain[...]
+    packed_out[9:10, :] = jnp.zeros((1, WIDE), f32)
+    for n in range(3):
+        packed_out[9:10, 128 * n : 128 * (n + 1)] = par[n, 0:1]
+    packed_out[9:10, 384 : 384 + STEPS] = losses
+
+
+def split_kernel(packed, loss_out, w_out, dec_out, bias_out, skip_out, gain_out):
+    w_out[...] = packed[0:8]
+    gain_out[...] = packed[8:9]
+    dec_out[...] = packed[9:10, 0:HEADS]
+    bias_out[...] = packed[9:10, 128 : 128 + HEADS]
+    skip_out[...] = packed[9:10, 256 : 256 + HEADS]
+    loss_out[...] = packed[9:10, 384 : 384 + STEPS]
 
 
 def per_device(x, z, bc, raw, ids, counts, target, weight, dec, bias, skip, gain):
     vmem = pl.BlockSpec(memory_space=pltpu.VMEM)
     smem = pl.BlockSpec(memory_space=pltpu.SMEM)
+    anywhere = pl.BlockSpec(memory_space=pl.ANY)
     shape = jax.ShapeDtypeStruct
-    outs = pl.pallas_call(
+    packed = pl.pallas_call(
         kernel,
-        out_shape=(
-            shape((1, STEPS), f32), shape((8, WIDE), f32), shape((1, HEADS), f32), shape((1, HEADS), f32),
-            shape((1, HEADS), f32), shape((1, WIDE), f32),
-        ),
-        in_specs=[vmem] * 5 + [smem] + [vmem] * 6,
-        out_specs=(vmem,) * 6,
+        out_shape=shape((16, WIDE), f32),
+        in_specs=[anywhere] * 3 + [vmem] * 2 + [smem] + [anywhere] + [vmem] * 5,
+        out_specs=vmem,
         scratch_shapes=list(scratch().values()),
         compiler_params=pltpu.CompilerParams(
             collective_id=0, has_side_effects=True, vmem_limit_bytes=62 * 1024 * 1024
         ),
     )(
-        x[0], z[0], bc[0], raw[0], ids, counts, target[0], weight,
+        x[0], z[0], bc[0], raw[0].T, ids, counts, target[0], weight,
         dec.reshape(1, HEADS), bias.reshape(1, HEADS), skip.reshape(1, HEADS), gain.reshape(1, WIDE),
     )
-    losses, weight, dec, bias, skip, gain = outs
+    losses, weight, dec, bias, skip, gain = pl.pallas_call(
+        split_kernel,
+        out_shape=(
+            shape((1, STEPS), f32), shape((8, WIDE), f32), shape((1, HEADS), f32), shape((1, HEADS), f32),
+            shape((1, HEADS), f32), shape((1, WIDE), f32),
+        ),
+        in_specs=[vmem],
+        out_specs=(vmem,) * 6,
+    )(packed)
     return (
         losses.reshape(STEPS), weight, dec.reshape(HEADS), bias.reshape(HEADS), skip.reshape(HEADS), gain.reshape(WIDE)
     )

time: 117 us -> 102 us (0.87)
  Pallas kernels: 110 us -> 101 us
  local copies, waits for them, and re-layouts: 6.17 us -> 0 us
    pallas_call x1 -> x2, Pallas kernels: 110 us -> 101 us  [the longest x1 99.1 us: per_device(): pl.pallas_call(kernel, out_shape=shape((16, WIDE), f32), in_specs=[anywhe...]
    unnamed x17 -> x0, local copies, waits for them, and re-layouts: 6.17 us -> none
where the time goes in v3:
time: 102 us; the launch traced here: 101 us
  Pallas kernels  101 us (99%)
    pallas_call x1, Pallas kernels, per_device(): pl.pallas_call(kernel, out_shape=shape((16, WIDE), f32), in_specs=[anywhe...  99.1 us

profile of v3, /device:TPU:1, one launch (start us, length us, event | category | flops | bytes accessed | tf_op | source)
XLA Modules:
  0.0 101.3 jit_solution(10907409901149740140)
XLA Ops:
  0.6 99.1 %shard_map.163.packed = f32[16,1024]{1,0:T(8,128)} custom-call(bf16[384,1024]{1,0:T(8,128)(2,1)} %bitcast.16, bf16[384,1024]{1,0:T(8,128)(2,1)} %bitcast.17, bf16[384,256]{1,0:T(8,128)(2,1)} %bitcast.19, f32[16,384]{1,0:T(8,128)} %bitcast.20, s32[1,384]{1,0:T(1,128)} %refs_4_.1, s32[8]{0:T(128)} %refs_5_.1, bf16[384,1024]{1,0:T(8,128)(2,1)} %bitcast.18, ...), custom_call_target="tpu_custom_call" | custom-call | tf_op jit(solution)/shard_map/pallas_call | solution.py:724
  99.8 1.5 %shard_map.164 = (f32[1,2]{1,0:T(1,128)}, f32[8,1024]{1,0:T(8,128)}, f32[1,16]{1,0:T(1,128)}, f32[1,16]{1,0:T(1,128)}, f32[1,16]{1,0:T(1,128)}, /*index=5*/f32[1,1024]{1,0:T(1,128)}) custom-call(f32[16,1024]{1,0:T(8,128)} %shard_map.163.packed), custom_call_target="tpu_custom_call" | custom-call | tf_op jit(solution)/shard_map/pallas_call | solution.py:737

commit v4 on v3

--- a/solution.py
+++ b/solution.py
@@ -71,7 +71,7 @@
 def scratch():
     dma, v = pltpu.SemaphoreType.DMA, pltpu.VMEM
     rows_f, wide_f, wide_b = v((TOK, 128), f32), v((TOK, WIDE), f32), v((TOK, WIDE), bf16)
-    states, sixteen = v((CHUNKS + 1, STATE, WIDE), f32), v((N_SEQ, 16, HALF), bf16)
+    states, sixteen = v((CHUNKS + 1, STATE, WIDE), f32), v((2, N_SEQ, 16, HALF // 2), bf16)
     small, small16, small8 = v((16, 128), f32), v((N_SEQ, 16, 128), f32), v((N_DP, 16, 128), f32)
     named = dict(
         x_ref=wide_b, z_ref=wide_b, bc_ref=v((TOK, 2 * STATE), bf16), tgt_ref=wide_b, s_in=dma((4,)),
@@ -94,8 +94,10 @@
         named["ra" + p] = v((3, N_SEQ, 16, w), bf16)
         named["mid" + p] = v((N_SEQ, 16, w), bf16)
         named["rb" + p] = v((N_SEQ, 16, w), bf16)
-    for name, count in dict(s_send=9, s_recv=9, s_ps=4, s_pr=4, g1s=3, g1r=3, g2s=3, g2r=3, g3s=3, g3r=3, r1s=3, r1r=3, r2s=3, r2r=3).items():
+    for name, count in dict(s_ps=4, s_pr=4, g1s=3, g1r=3, g2s=3, g2r=3, g3s=3, g3r=3, r1s=3, r1r=3, r2s=3, r2r=3).items():
         named[name] = dma((count,))
+    named["s_send"] = dma((9, 2))
+    named["s_recv"] = dma((9, 2))
     return named
 
 
@@ -212,14 +214,14 @@
     def index_in(p, y, x, z):
         return {"y": y * 16 + x * 4 + z, "x": x * 16 + y * 4 + z, "z": z * 16 + x * 4 + y}[p]
 
-    def plane_peer(p, k):
-        a, b = {"y": (xx, zz), "x": (yy, zz), "z": (xx, yy)}[p]
-        q = (a * 4 + b + k) % 16
+    plane_far = sorted([(a, b) for a in range(4) for b in range(4)][1:], key=lambda offset: -hops(offset))
+
+    def plane_peer(p, a, b):
         if p == "y":
-            return dp, q, q
+            return dp, seqs[a, b], seqs[a, b]
         if p == "x":
-            return (q // 4) * 2 + core, xx * 4 + q % 4, q
-        return (q % 4) * 2 + core, (q // 4) * 4 + zz, q
+            return dps[a], seqs[0, b], ((yy + a) % 4) * 4 + (zz + b) % 4
+        return dps[b], seqs[a, 0], ((xx + a) % 4) * 4 + (yy + b) % 4
 
     def line_peer(p, k):
         c = (place[p] + k) % 4
@@ -239,12 +241,9 @@
             own = core * 64 + mine_in[p]
             buf[own] = jnp.concatenate([wown[:, lanes], wown[:, right]], axis=0).astype(bf16)
 
-            def send(k, carry):
-                d, s, _ = plane_peer(p, k)
+            for a, b in plane_far:
+                d, s, _ = plane_peer(p, a, b)
                 remote(buf.at[own], buf.at[own], g1s.at[n], g1r.at[n], d, s).start()
-                return carry
-
-            lax.fori_loop(1, 16, send, 0)
 
     def ag_line():
         for n, p in enumerate(PARTS):
@@ -298,40 +297,29 @@
                 piece = buf.at[pl.ds(0, count)]
                 remote(piece, piece, ss.at[n], rs.at[n], partner, seq).wait_send()
 
-    def exchange_start(src, dst, n):
-        def send(k, carry):
-            peer = (seq + k) % N_SEQ
-            remote(src.at[peer], dst.at[seq], s_send.at[n], s_recv.at[n], dp, peer).start()
-            return carry
-
-        lax.fori_loop(1, N_SEQ, send, 0)
-        dst[seq] = src[seq]
+    def exchange_start(src, dst, n, h):
+        for a, b in plane_far:
+            peer = seqs[a, b]
+            remote(src.at[h, peer], dst.at[h, seq], s_send.at[n, h], s_recv.at[n, h], dp, peer).start()
+        dst[h, seq] = src[h, seq]
 
     def spread_start(src, dst, n):
-        def send(k, carry):
-            peer = (seq + k) % N_SEQ
-            remote(src, dst.at[seq], s_send.at[n], s_recv.at[n], dp, peer).start()
-            return carry
-
-        lax.fori_loop(1, N_SEQ, send, 0)
+        for a, b in plane_far:
+            remote(src, dst.at[seq], s_send.at[n, 0], s_recv.at[n, 0], dp, seqs[a, b]).start()
         dst[seq] = src[...]
 
     def cross_start(src, dst, n):
-        def send(k, carry):
-            peer = (dp + k) % N_DP
-            remote(src, dst.at[dp], s_send.at[n], s_recv.at[n], peer, seq).start()
-            return carry
-
-        lax.fori_loop(1, N_DP, send, 0)
+        for k in range(1, N_DP):
+            remote(src, dst.at[dp], s_send.at[n, 0], s_recv.at[n, 0], (dp + k) % N_DP, seq).start()
         dst[dp] = src[...]
 
-    def recv_wait(dst, n, count):
+    def recv_wait(dst, n, count, h=0):
         piece = dst.at[pl.ds(0, count)]
-        remote(piece, piece, s_send.at[n], s_recv.at[n], partner, seq).wait_recv()
-
-    def send_wait(dst, n, count):
+        remote(piece, piece, s_send.at[n, h], s_recv.at[n, h], partner, seq).wait_recv()
+
+    def send_wait(dst, n, count, h=0):
         piece = dst.at[pl.ds(0, count)]
-        remote(piece, piece, s_send.at[n], s_recv.at[n], partner, seq).wait_send()
+        remote(piece, piece, s_send.at[n, h], s_recv.at[n, h], partner, seq).wait_send()
 
     def one_step(step, losses):
         dec_t, bias_t, skip_t = par[0, 0:1], par[1, 0:1], par[2, 0:1]
@@ -372,7 +360,16 @@
         def to_blocks(state, out):
             for r in range(8):
                 for h in range(2):
-                    out[2 * r + h] = state[16 * r : 16 * r + 16, HALF * h : HALF * (h + 1)].astype(bf16)
+                    for q in range(2):
+                        first = HALF * h + 256 * q
+                        out[q, 2 * r + h] = state[16 * r : 16 * r + 16, first : first + 256].astype(bf16)
+
+        def from_blocks(source, put):
+            for q in range(2):
+                for r in range(8):
+                    for h in range(2):
+                        first = HALF * h + 256 * q
+                        put(slice(16 * r, 16 * r + 16), slice(first, first + 256), source[q, 2 * r + h].astype(f32))
 
         to_blocks(hst[0], hs)
 
@@ -390,8 +387,9 @@
             pl.semaphore_wait(barrier, 67)
             ag_start()
 
-        exchange_start(hs, hr, 0)
+        exchange_start(hs, hr, 0, 0)
         spread_start(cs, cr, 1)
+        exchange_start(hs, hr, 0, 1)
 
         def inside(c, carry):
             s = dec_s[rows(c)]
@@ -414,30 +412,29 @@
 
         half = seq % 2
 
-        def carry_rows(i):
-            return [cr[i, pl.ds(4 * half + m, 1), :] for m in range(4)]
-
-        recv_wait(hr, 0, 15)
+        def scan(source, out, h, order):
+            state = [jnp.zeros((16, 128), f32) for _ in range(2)]
+            for i in order:
+                for m in range(2):
+                    lanes = slice(128 * m, 128 * (m + 1))
+                    out[h, i, :, lanes] = state[m].astype(bf16)
+                    factor = cr[i, pl.ds(4 * half + 2 * h + m, 1), :]
+                    state[m] = factor * state[m] + source[h, i, :, lanes].astype(f32)
+
         recv_wait(cr, 1, 15)
-
-        def forward(i, state):
-            factors = carry_rows(i)
-            out = []
-            for m in range(4):
-                lanes = slice(128 * m, 128 * (m + 1))
-                hp[i, :, lanes] = state[m].astype(bf16)
-                out.append(factors[m] * state[m] + hr[i, :, lanes].astype(f32))
-            return tuple(out)
-
-        zeros4 = tuple(jnp.zeros((16, 128), f32) for _ in range(4))
-        lax.fori_loop(0, N_SEQ, forward, zeros4)
-        exchange_start(hp, hi, 2)
+        for h in range(2):
+            recv_wait(hr.at[h], 0, 15, h)
+            scan(hr, hp, h, range(N_SEQ))
+            exchange_start(hp, hi, 2, h)
         ag_cross()
         ag_finish()
-        recv_wait(hi, 2, 15)
-        for r in range(8):
-            for h in range(2):
-                hst[0, 16 * r : 16 * r + 16, HALF * h : HALF * (h + 1)] = hi[2 * r + h].astype(f32)
+        for h in range(2):
+            recv_wait(hi.at[h], 2, 15, h)
+
+        def put_state(at_rows, lanes, value):
+            hst[0, at_rows, lanes] = value
+
+        from_blocks(hi, put_state)
 
         skip_e = expand(jnp.broadcast_to(skip_t, (8, 128)))[0:1]
         gain_e = gain[...]
@@ -484,16 +481,21 @@
             apart[c] = dot_tn(bc_ref[span, STATE:], (g * eexp[span]).astype(bf16))
         entry = apart[0] + chain[0:1] * (apart[1] + chain[1:2] * apart[2])
         to_blocks(entry, gs)
-        exchange_start(gs, gr, 3)
-        def grad_rows(d):
-            lanes = pl.ds(pl.multiple_of(d * 128, 128), 128)
-            return blocks_of(dot_tn(normb[:, lanes], ogb[...]))
-
-        for k in (1, 2, 3, 0):
-            y_k = (yy + k) % N_Y
-            d = y_k * 2 + 1 - core
-            wgp[k] = grad_rows(d).astype(bf16)
-            remote(wgp.at[k], pr.at[k], s_ps.at[k], s_pr.at[k], partner, seq).start()
+        for h in range(2):
+            exchange_start(gs, gr, 3, h)
+        def grad_rows(first, second):
+            lanes = [normb[:, pl.ds(pl.multiple_of(d * 128, 128), 128)] for d in (first, second)]
+            both = dot_tn(jnp.concatenate(lanes, axis=1), ogb[...])
+            return blocks_of(both[:128]), blocks_of(both[128:])
+
+        def group(k, c):
+            return ((yy + k) % N_Y) * 2 + c
+
+        for pair in ((1, 2), (3, 0)):
+            pieces = grad_rows(*[group(k, 1 - core) for k in pair])
+            for k, piece in zip(pair, pieces):
+                wgp[k] = piece.astype(bf16)
+                remote(wgp.at[k], pr.at[k], s_ps.at[k], s_pr.at[k], partner, seq).start()
         gain_g = jnp.sum(accs[0], axis=0, keepdims=True)
         for r in range(8):
             sa[r : r + 1, :] = gain_g[:, 128 * r : 128 * (r + 1)]
@@ -502,23 +504,24 @@
         sa[8:16, :] = jnp.where(sub == 0, skip_g, jnp.where(sub == 1, jnp.broadcast_to(loss, (8, 128)), 0.0))
         spread_start(sa, sar, 4)
 
-        for k in (1, 2, 3, 0):
-            y_k = (yy + k) % N_Y
-            mine = grad_rows(y_k * 2 + core)
-            remote(wgp.at[k], pr.at[k], s_ps.at[k], s_pr.at[k], partner, seq).wait_recv()
-            both = (mine + pr[k].astype(f32)).astype(bf16)
-            part["sby"][pl.ds(y_k * 16, 16)] = both[:, :, : WIDTH["y"]]
-            if k > 0:
-                slab = part["sby"].at[pl.ds(y_k * 16, 16)]
-                remote(slab, part["ray"].at[k - 1], r1s.at[0], r1r.at[0], y_k * 2 + core, seq).start()
-            for p in "xz":
-                piece = both[:, :, FIRST[p] : FIRST[p] + WIDTH[p]]
-                for x in range(4):
-                    if p == "x":
-                        part["sbx"][pl.ds(x * 16 + y_k * 4, 4)] = piece[4 * x : 4 * x + 4]
-                    else:
-                        for z in range(4):
-                            part["sbz"][z * 16 + x * 4 + y_k] = piece[4 * x + z]
+        for pair in ((1, 2), (3, 0)):
+            pieces = grad_rows(*[group(k, core) for k in pair])
+            for k, mine in zip(pair, pieces):
+                y_k = (yy + k) % N_Y
+                remote(wgp.at[k], pr.at[k], s_ps.at[k], s_pr.at[k], partner, seq).wait_recv()
+                both = (mine + pr[k].astype(f32)).astype(bf16)
+                part["sby"][pl.ds(y_k * 16, 16)] = both[:, :, : WIDTH["y"]]
+                if k > 0:
+                    slab = part["sby"].at[pl.ds(y_k * 16, 16)]
+                    remote(slab, part["ray"].at[k - 1], r1s.at[0], r1r.at[0], y_k * 2 + core, seq).start()
+                for p in "xz":
+                    piece = both[:, :, FIRST[p] : FIRST[p] + WIDTH[p]]
+                    for x in range(4):
+                        if p == "x":
+                            part["sbx"][pl.ds(x * 16 + y_k * 4, 4)] = piece[4 * x : 4 * x + 4]
+                        else:
+                            for z in range(4):
+                                part["sbz"][z * 16 + x * 4 + y_k] = piece[4 * x + z]
         for n, p in ((1, "x"), (2, "z")):
             for k in range(1, 4):
                 d, s, c = line_peer(p, k)
@@ -526,26 +529,18 @@
                 remote(slab, part["ra" + p].at[k - 1], r1s.at[n], r1r.at[n], d, s).start()
 
         def scatter_plane():
-            for n, p in enumerate(PARTS):
+            for p in "xzy":
+                n = PARTS.index(p)
                 got, mid, dst = part["ra" + p], part["mid" + p], part["rb" + p]
                 remote(got, got, r1s.at[n], r1r.at[n], partner, seq).wait_recv()
-
-                def add(j, carry):
-                    value = part["sb" + p][place[p] * 16 + j].astype(f32)
-                    for k in range(3):
-                        value = value + got[k, j].astype(f32)
-                    mid[j] = value.astype(bf16)
-                    return carry
-
-                lax.fori_loop(0, 16, add, 0)
+                value = part["sb" + p][pl.ds(place[p] * 16, 16)].astype(f32)
+                for k in range(3):
+                    value = value + got[k].astype(f32)
+                mid[...] = value.astype(bf16)
                 here = mine_in[p] % 16
-
-                def send(k, carry):
-                    d, s, q = plane_peer(p, k)
+                for a, b in plane_far:
+                    d, s, q = plane_peer(p, a, b)
                     remote(mid.at[q], dst.at[here], r2s.at[n], r2r.at[n], d, s).start()
-                    return carry
-
-                lax.fori_loop(1, 16, send, 0)
                 dst[here] = mid[here]
 
         def inside_back(c, carry):
@@ -567,20 +562,10 @@
 
         lax.fori_loop(0, CHUNKS, inside_back, 0)
 
-        recv_wait(gr, 3, 15)
-
-        def backward(n, state):
-            i = N_SEQ - 1 - n
-            factors = carry_rows(i)
-            out = []
-            for m in range(4):
-                lanes = slice(128 * m, 128 * (m + 1))
-                gp[i, :, lanes] = state[m].astype(bf16)
-                out.append(factors[m] * state[m] + gr[i, :, lanes].astype(f32))
-            return tuple(out)
-
-        lax.fori_loop(0, N_SEQ, backward, zeros4)
-        exchange_start(gp, gi, 5)
+        for h in range(2):
+            recv_wait(gr.at[h], 3, 15, h)
+            scan(gr, gp, h, range(N_SEQ - 1, -1, -1))
+            exchange_start(gp, gi, 5, h)
 
         scatter_plane()
 
@@ -594,11 +579,13 @@
         sb2[...] = summed(sar, N_SEQ)
         cross_start(sb2, sbr, 6)
 
-        recv_wait(gi, 5, 15)
-        for r in range(8):
-            for h in range(2):
-                apart[3, 16 * r : 16 * r + 16, HALF * h : HALF * (h + 1)] = gi[2 * r + h].astype(f32)
-
+        for h in range(2):
+            recv_wait(gi.at[h], 5, 15, h)
+
+        def put_after(at_rows, lanes, value):
+            apart[3, at_rows, lanes] = value
+
+        from_blocks(gi, put_after)
         apart[2] = apart[2] + chain[2:3] * apart[3]
         apart[1] = apart[1] + chain[1:2] * apart[2]
 
@@ -640,13 +627,13 @@
             grad[p] = value
             square = square + jnp.sum(jnp.sum(value * value, axis=1, keepdims=True), axis=0, keepdims=True)
         t1[...] = jnp.where(lane < 16, dec_g, jnp.where(lane < 32, bias_g, jnp.where(lane == 32, square, 0.0)))
-        pair = remote(t1, t1r, s_send.at[7], s_recv.at[7], partner, seq)
+        pair = remote(t1, t1r, s_send.at[7, 0], s_recv.at[7, 0], partner, seq)
         pair.start()
         pair.wait_recv()
         t2[...] = t1[...] + t1r[...]
 
         for a, b, c in far_first:
-            remote(t2, t2r.at[own_q], s_send.at[8], s_recv.at[8], dps[a], seqs[b, c]).start()
+            remote(t2, t2r.at[own_q], s_send.at[8, 0], s_recv.at[8, 0], dps[a], seqs[b, c]).start()
         t2r[own_q] = t2[...]
         recv_wait(t2r, 8, 63)
         sums_b = jnp.sum(t2r[...], axis=0)
@@ -675,12 +662,16 @@
                 lanes = slice(HALF * h + FIRST[p], HALF * h + FIRST[p] + WIDTH[p])
                 wown[:, lanes] = wown[:, lanes] - move * grad[p][8 * h : 8 * h + 8]
 
-        send_wait(hr, 0, 15)
+        for h in range(2):
+            send_wait(hr.at[h], 0, 15, h)
         send_wait(cr, 1, 15)
-        send_wait(hi, 2, 15)
-        send_wait(gr, 3, 15)
+        for h in range(2):
+            send_wait(hi.at[h], 2, 15, h)
+        for h in range(2):
+            send_wait(gr.at[h], 3, 15, h)
         send_wait(sar, 4, 15)
-        send_wait(gi, 5, 15)
+        for h in range(2):
+            send_wait(gi.at[h], 5, 15, h)
         send_wait(sbr, 6, 7)
         pair.wait_send()
         send_wait(t2r, 8, 63)

time: 102 us -> 97.1 us (0.952)
  Pallas kernels: 101 us -> 96.3 us
    pallas_call x1, Pallas kernels: 99.1 us -> 94.8 us  [per_device(): pl.pallas_call(kernel, out_shape=shape((16, WIDE), f32), in_specs=[anywhe...]
where the time goes in v4:
time: 97.1 us; the launch traced here: 96.9 us
  Pallas kernels  96.3 us (99%)
    pallas_call x1, Pallas kernels, per_device(): pl.pallas_call(kernel, out_shape=shape((16, WIDE), f32), in_specs=[anywhe...  94.8 us

profile of v4, /device:TPU:1, one launch (start us, length us, event | category | flops | bytes accessed | tf_op | source)
XLA Modules:
  0.0 96.9 jit_solution(15636947137868081605)
XLA Ops:
  0.6 94.8 %shard_map.163.packed = f32[16,1024]{1,0:T(8,128)} custom-call(bf16[384,1024]{1,0:T(8,128)(2,1)} %bitcast.16, bf16[384,1024]{1,0:T(8,128)(2,1)} %bitcast.17, bf16[384,256]{1,0:T(8,128)(2,1)} %bitcast.19, f32[16,384]{1,0:T(8,128)} %bitcast.20, s32[1,384]{1,0:T(1,128)} %refs_4_.1, s32[8]{0:T(128)} %refs_5_.1, bf16[384,1024]{1,0:T(8,128)(2,1)} %bitcast.18, ...), custom_call_target="tpu_custom_call" | custom-call | tf_op jit(solution)/shard_map/pallas_call | solution.py:715
  95.4 1.5 %shard_map.164 = (f32[1,2]{1,0:T(1,128)}, f32[8,1024]{1,0:T(8,128)}, f32[1,16]{1,0:T(1,128)}, f32[1,16]{1,0:T(1,128)}, f32[1,16]{1,0:T(1,128)}, /*index=5*/f32[1,1024]{1,0:T(1,128)}) custom-call(f32[16,1024]{1,0:T(8,128)} %shard_map.163.packed), custom_call_target="tpu_custom_call" | custom-call | tf_op jit(solution)/shard_map/pallas_call | solution.py:728

commit v5 on v4

--- a/solution.py
+++ b/solution.py
@@ -75,7 +75,7 @@
     small, small16, small8 = v((16, 128), f32), v((N_SEQ, 16, 128), f32), v((N_DP, 16, 128), f32)
     named = dict(
         x_ref=wide_b, z_ref=wide_b, bc_ref=v((TOK, 2 * STATE), bf16), tgt_ref=wide_b, s_in=dma((4,)),
-        act=wide_f, gat=wide_f, dnf=wide_f, invs=rows_f,
+        act=wide_f, gat=wide_f, dnf=wide_f, gdn=wide_f, invs=rows_f,
         ex=v((128, WIDE), bf16), red=v((WIDE, 128), bf16), tri=v((CHUNK, CHUNK), f32), par=v((3, 8, 128), f32),
         gain=v((1, WIDE), f32), wown=v((8, WIDE), f32), rawt=rows_f, wid=rows_f, dec_s=rows_f, ent=rows_f,
         chain=v((8, WIDE), f32), fcol=v((CHUNKS, CHUNK, CHUNK), f32), sc=v((CHUNKS, CHUNK, CHUNK), f32),
@@ -84,8 +84,8 @@
         hs=sixteen, hr=sixteen, hp=sixteen, hi=sixteen, gs=sixteen, gr=sixteen, gp=sixteen, gi=sixteen,
         cs=v((8, 128), f32), cr=v((N_SEQ, 8, 128), f32), wfull=v((WIDE, WIDE), bf16),
         wgp=v((N_Y, N_SEQ, 16, HALF), bf16), pr=v((N_Y, N_SEQ, 16, HALF), bf16),
-        sa=small, sar=small16, sb2=small, sbr=small8, t1=v((1, 128), f32), t1r=v((1, 128), f32), t2=v((1, 128), f32),
-        t2r=v((64, 1, 128), f32),
+        sa=small, sar=small16, sb2=small, sbr=small8, t1=v((1, 128), f32),
+        t2r=v((128, 1, 128), f32),
     )
     for p in PARTS:
         w = WIDTH[p]
@@ -109,16 +109,16 @@
 
 def program(
     x_in, z_in, bc_in, raw_in, ids_ref, cnt_ref, tgt_in, w_ref, dec_in, bias_in, skip_in, gain_in,
-    packed_out, x_ref, z_ref, bc_ref, tgt_ref, s_in, act, gat, dnf, invs,
+    packed_out, x_ref, z_ref, bc_ref, tgt_ref, s_in, act, gat, dnf, gdn, invs,
     ex, red, tri, par, gain, wown, rawt, wid, dec_s, ent, chain, fcol, sc,
     xw, wtd, yin, eexp, gstate, hst, apart, normb, ogb, gb, q2a, ds1, accs,
-    hs, hr, hp, hi, gs, gr, gp, gi, cs, cr, wfull, wgp, pr, sa, sar, sb2, sbr, t1, t1r, t2, t2r,
+    hs, hr, hp, hi, gs, gr, gp, gi, cs, cr, wfull, wgp, pr, sa, sar, sb2, sbr, t1, t2r,
     s_send, s_recv, s_ps, s_pr, g1s, g1r, g2s, g2r, g3s, g3r, r1s, r1r, r2s, r2r, **part,
 ):
     dp, seq = lax.axis_index(DP), lax.axis_index(SEQ)
     yy, core = dp // 2, dp % 2
     partner = dp + 1 - 2 * core
-    own_q = yy * N_SEQ + seq
+    own_b = dp * N_SEQ + seq
     xx, zz = seq // 4, seq % 4
     place = {"y": yy, "x": xx, "z": zz}
     MESH = pl.DeviceIdType.MESH
@@ -141,10 +141,13 @@
 
     chips = [(a, b, c) for a in range(4) for b in range(4) for c in range(4)]
     far_first = sorted(chips[1:], key=lambda offset: -hops(offset))
-    for a, b, c in far_first:
-        pl.semaphore_signal(barrier, 1, device_id=at(dps[a], seqs[b, c]), device_id_type=MESH)
-    for k in range(4):
-        pl.semaphore_signal(barrier, 1, device_id=at(dps[k] + 1 - 2 * core, seq), device_id_type=MESH)
+    everyone = []
+    for a, b, c in far_first + chips[:1]:
+        for flip in (0, 1):
+            if (a, b, c, flip) != (0, 0, 0, 0):
+                everyone.append((dps[a] + flip * (1 - 2 * core), seqs[b, c]))
+    for d, s in everyone:
+        pl.semaphore_signal(barrier, 1, device_id=at(d, s), device_id_type=MESH)
     loads = [
         pltpu.make_async_copy(source, target, s_in.at[n])
         for n, (source, target) in enumerate(((bc_in, bc_ref), (x_in, x_ref), (z_in, z_ref), (tgt_in, tgt_ref)))
@@ -202,10 +205,7 @@
         flag = jnp.where(ids_ref[0:1, rows(c)] == 0, 1.0, 0.0)
         flag_col = jnp.broadcast_to(flag, (CHUNK, CHUNK)).T
         seg = dot(tri[...], flag_col)
-        seg_row = seg.T
         fcol[c] = seg
-        scores = dot_nt(bc_ref[rows(c), STATE:], bc_ref[rows(c), :STATE])
-        sc[c] = jnp.where((seg == seg_row) & (ti >= tj), scores, 0.0)
         return carry
 
     lax.fori_loop(0, CHUNKS, prepare, 0)
@@ -255,40 +255,41 @@
                 d, s, _ = line_peer(p, k)
                 remote(slab, slab, g2s.at[n], g2r.at[n], d, s).start()
 
-    def ag_cross():
-        for n, p in enumerate(PARTS):
-            buf = part["ag" + p]
+    def unpack(p, its_core):
+        buf, w, base = part["ag" + p], WIDTH[p], its_core * 64
+
+        def one(y, carry):
+            d = y * 2 + its_core
+            if p == "y":
+                blocks = [buf[pl.ds(base + y * 16, 16)].astype(f32)]
+            elif p == "x":
+                blocks = [buf[pl.ds(base + x * 16 + y * 4, 4)].astype(f32) for x in range(4)]
+            else:
+                blocks = [buf[pl.ds(base + z * 16 + x * 4 + y, 1)].astype(f32) for x in range(4) for z in range(4)]
+            tops, lows = [], []
+            for block in blocks:
+                split = block.reshape(block.shape[0], 2, 8, w)
+                tops.append(split[:, 0].reshape(-1, w))
+                lows.append(split[:, 1].reshape(-1, w))
+            wfull[rows(d), FIRST[p] : FIRST[p] + w] = jnp.concatenate(tops, axis=0).astype(bf16)
+            wfull[rows(d), HALF + FIRST[p] : HALF + FIRST[p] + w] = jnp.concatenate(lows, axis=0).astype(bf16)
+            return carry
+
+        lax.fori_loop(0, N_Y, one, 0)
+
+    def ag_finish():
+        for p in "xzy":
+            n, buf = PARTS.index(p), part["ag" + p]
             piece = buf.at[pl.ds(0, 48)]
             remote(piece, piece, g2s.at[n], g2r.at[n], partner, seq).wait_recv()
             ours = buf.at[pl.ds(core * 64, 64)]
             remote(ours, ours, g3s.at[n], g3r.at[n], partner, seq).start()
-
-    def ag_finish():
-        def unpack(y, its_core):
-            base, d = its_core * 64, y * 2 + its_core
-            for p in PARTS:
-                buf, w = part["ag" + p], WIDTH[p]
-                if p == "y":
-                    blocks = [buf[pl.ds(base + y * 16, 16)].astype(f32)]
-                elif p == "x":
-                    blocks = [buf[pl.ds(base + x * 16 + y * 4, 4)].astype(f32) for x in range(4)]
-                else:
-                    blocks = [buf[pl.ds(base + z * 16 + x * 4 + y, 1)].astype(f32) for x in range(4) for z in range(4)]
-                tops, lows = [], []
-                for block in blocks:
-                    split = block.reshape(block.shape[0], 2, 8, w)
-                    tops.append(split[:, 0].reshape(-1, w))
-                    lows.append(split[:, 1].reshape(-1, w))
-                wfull[rows(d), FIRST[p] : FIRST[p] + w] = jnp.concatenate(tops, axis=0).astype(bf16)
-                wfull[rows(d), HALF + FIRST[p] : HALF + FIRST[p] + w] = jnp.concatenate(lows, axis=0).astype(bf16)
-            return its_core
-
-        lax.fori_loop(0, N_Y, unpack, core)
-        for n, p in enumerate(PARTS):
-            buf = part["ag" + p]
+            unpack(p, core)
+        for p in "xzy":
+            n, buf = PARTS.index(p), part["ag" + p]
             piece = buf.at[pl.ds((1 - core) * 64, 64)]
             remote(piece, piece, g3s.at[n], g3r.at[n], partner, seq).wait_recv()
-        lax.fori_loop(0, N_Y, unpack, 1 - core)
+            unpack(p, 1 - core)
 
     def ag_sent():
         for n, p in enumerate(PARTS):
@@ -375,21 +376,29 @@
 
         @pl.when(step == 0)
         def _():
-            loads[2].wait()
-
-            def activate(c, carry):
-                z_f = z_ref[rows(c)].astype(f32)
-                act[rows(c)] = z_f / (1.0 + jnp.exp(-z_f))
-                return carry
-
-            lax.fori_loop(0, CHUNKS, activate, 0)
-            loads[3].wait()
-            pl.semaphore_wait(barrier, 67)
+            pl.semaphore_wait(barrier, 127)
             ag_start()
 
         exchange_start(hs, hr, 0, 0)
         spread_start(cs, cr, 1)
         exchange_start(hs, hr, 0, 1)
+
+        @pl.when(step == 0)
+        def _():
+            loads[2].wait()
+
+            def once(c, carry):
+                z_f = z_ref[rows(c)].astype(f32)
+                act[rows(c)] = z_f / (1.0 + jnp.exp(-z_f))
+                scores = dot_nt(bc_ref[rows(c), STATE:], bc_ref[rows(c), :STATE])
+                sc[c] = jnp.where((fcol[c] == fcol[c].T) & (ti >= tj), scores, 0.0)
+                return carry
+
+            lax.fori_loop(0, CHUNKS, once, 0)
+            loads[3].wait()
+
+        skip_e = expand(jnp.broadcast_to(skip_t, (8, 128)))[0:1]
+        gain_e = gain[...]
 
         def inside(c, carry):
             s = dec_s[rows(c)]
@@ -404,7 +413,9 @@
                     parts.append((jnp.exp(gap) * scores).astype(bf16))
                 mine = xw[rows(c), 128 * p : 128 * (p + 1)]
                 both = jnp.concatenate([mine * low_half, mine * high_half], axis=0)
-                yin[rows(c), 128 * p : 128 * (p + 1)] = dot(jnp.concatenate(parts, axis=1), both)
+                lanes = slice(128 * p, 128 * (p + 1))
+                direct = skip_e[:, lanes] * x_ref[rows(c), lanes].astype(f32)
+                yin[rows(c), lanes] = dot(jnp.concatenate(parts, axis=1), both) + direct
             return carry
 
         lax.fori_loop(0, CHUNKS, inside, 0)
@@ -426,7 +437,6 @@
             recv_wait(hr.at[h], 0, 15, h)
             scan(hr, hp, h, range(N_SEQ))
             exchange_start(hp, hi, 2, h)
-        ag_cross()
         ag_finish()
         for h in range(2):
             recv_wait(hi.at[h], 2, 15, h)
@@ -436,48 +446,46 @@
 
         from_blocks(hi, put_state)
 
-        skip_e = expand(jnp.broadcast_to(skip_t, (8, 128)))[0:1]
-        gain_e = gain[...]
         scale = 2.0 / (WIDE * total_f)
-        accs[1] = jnp.zeros((8, WIDE), f32)
+        accs[...] = jnp.zeros(accs.shape, f32)
 
         for c in range(CHUNKS):
             span = slice(c * CHUNK, (c + 1) * CHUNK)
             state = hst[c]
-            y_sum = yin[span] + eexp[span] * dot(bc_ref[span, STATE:], state.astype(bf16))
-            yin[span] = y_sum
-            gated = (y_sum + skip_e * x_ref[span].astype(f32)) * act[span]
+            y = yin[span] + eexp[span] * dot(bc_ref[span, STATE:], state.astype(bf16))
+            yin[span] = y
+            gated = y * act[span]
             gat[span] = gated
             inv = lax.rsqrt(jnp.sum(gated * gated, axis=1, keepdims=True) * (1.0 / WIDE) + norm_floor)
             invs[span] = jnp.broadcast_to(inv, (CHUNK, 128))
             normb[span] = (gated * gain_e * inv).astype(bf16)
             hst[c + 1] = chain[c : c + 1] * state + gstate[c]
-        position = seq * TOK + iota((TOK, 256), 0)
+        block = 512
+        position = seq * TOK + iota((TOK, block), 0)
         scored = jnp.where(position < own_count, 1.0, 0.0)
-        losses_8 = jnp.zeros((8, 256), f32)
-        for n in range(4):
-            lanes = slice(256 * n, 256 * (n + 1))
+        losses_8 = jnp.zeros((8, block), f32)
+        for first in range(0, WIDE, block):
+            lanes = slice(first, first + block)
             res = (dot(normb[...], wfull[:, lanes]) - tgt_ref[:, lanes].astype(f32)) * scored
-            losses_8 = losses_8 + jnp.sum((res * res).reshape(TOK // 8, 8, 256), axis=0)
+            losses_8 = losses_8 + jnp.sum((res * res).reshape(TOK // 8, 8, block), axis=0)
             ogb[:, lanes] = (res * scale).astype(bf16)
         loss = jnp.sum(jnp.sum(losses_8, axis=1, keepdims=True), axis=0, keepdims=True)
         inner_l = jnp.zeros((TOK, 128), f32)
-        for n in range(4):
-            lanes = slice(256 * n, 256 * (n + 1))
+        for first in range(0, WIDE, block):
+            lanes = slice(first, first + block)
             d_norm = dot_nt(ogb[...], wfull[lanes, :])
             dnf[:, lanes] = d_norm
-            inv_2 = jnp.concatenate([invs[...], invs[...]], axis=1)
-            d_gr = d_norm * gat[:, lanes] * inv_2
-            accs[0, :, lanes] = jnp.sum(d_gr.reshape(TOK // 8, 8, 256), axis=0)
-            term = d_gr * gain_e[:, lanes]
-            inner_l = inner_l + (term[:, :128] + term[:, 128:])
+            d_gain = d_norm * gain_e[:, lanes]
+            gdn[:, lanes] = d_gain
+            term = d_gain * gat[:, lanes]
+            for k in range(0, block, 128):
+                inner_l = inner_l + term[:, k : k + 128]
         inner = jnp.sum(inner_l, axis=1, keepdims=True) * (1.0 / WIDE)
         for c in range(CHUNKS):
             span = slice(c * CHUNK, (c + 1) * CHUNK)
             inv = invs[span, 0:1]
-            g = inv * (gain_e * dnf[span] - gat[span] * (inv * inner[span])) * act[span]
+            g = (gdn[span] - gat[span] * (inv * inv * inner[span])) * inv * act[span]
             gb[span] = g.astype(bf16)
-            accs[1] += jnp.sum((g * x_ref[span].astype(f32)).reshape(16, 8, WIDE), axis=0)
             apart[c] = dot_tn(bc_ref[span, STATE:], (g * eexp[span]).astype(bf16))
         entry = apart[0] + chain[0:1] * (apart[1] + chain[1:2] * apart[2])
         to_blocks(entry, gs)
@@ -496,6 +504,13 @@
             for k, piece in zip(pair, pieces):
                 wgp[k] = piece.astype(bf16)
                 remote(wgp.at[k], pr.at[k], s_ps.at[k], s_pr.at[k], partner, seq).start()
+        def small_sums(c, carry):
+            x_f, inv = x_ref[rows(c)].astype(f32), invs[rows(c), 0:1]
+            accs[0] += jnp.sum((dnf[rows(c)] * gat[rows(c)] * inv).reshape(16, 8, WIDE), axis=0)
+            accs[1] += jnp.sum((gb[rows(c)].astype(f32) * x_f).reshape(16, 8, WIDE), axis=0)
+            return carry
+
+        lax.fori_loop(0, CHUNKS, small_sums, 0)
         gain_g = jnp.sum(accs[0], axis=0, keepdims=True)
         for r in range(8):
             sa[r : r + 1, :] = gain_g[:, 128 * r : 128 * (r + 1)]
@@ -503,7 +518,6 @@
         sub = iota((8, 128), 0)
         sa[8:16, :] = jnp.where(sub == 0, skip_g, jnp.where(sub == 1, jnp.broadcast_to(loss, (8, 128)), 0.0))
         spread_start(sa, sar, 4)
-
         for pair in ((1, 2), (3, 0)):
             pieces = grad_rows(*[group(k, core) for k in pair])
             for k, mine in zip(pair, pieces):
@@ -556,16 +570,18 @@
                 both = jnp.concatenate([mine * low_half, mine * high_half], axis=0)
                 lanes = slice(128 * p, 128 * (p + 1))
                 eexp[rows(c), lanes] = dot(jnp.concatenate(parts, axis=1), both)
-            ds1[rows(c)] = head_sum(gb[rows(c)].astype(f32) * yin[rows(c)])
+            g_f, x_f = gb[rows(c)].astype(f32), x_ref[rows(c)].astype(f32)
+            ds1[rows(c)] = head_sum(g_f * (yin[rows(c)] - skip_e * x_f))
             q2a[rows(c)] = head_sum(xw[rows(c)].astype(f32) * eexp[rows(c)])
             return carry
 
-        lax.fori_loop(0, CHUNKS, inside_back, 0)
+        lax.fori_loop(0, CHUNKS - 1, inside_back, 0)
 
         for h in range(2):
             recv_wait(gr.at[h], 3, 15, h)
             scan(gr, gp, h, range(N_SEQ - 1, -1, -1))
             exchange_start(gp, gi, 5, h)
+        lax.fori_loop(CHUNKS - 1, CHUNKS, inside_back, 0)
 
         scatter_plane()
 
@@ -589,27 +605,22 @@
         apart[2] = apart[2] + chain[2:3] * apart[3]
         apart[1] = apart[1] + chain[1:2] * apart[2]
 
-        def back(c, sums):
-            dec_g, bias_g = sums
+        dec_g = bias_g = jnp.zeros((1, 128), f32)
+        sig = 1.0 / (1.0 + jnp.exp(-(rawt[...] + bias_t)))
+        for c in range(CHUNKS):
+            span = slice(c * CHUNK, (c + 1) * CHUNK)
             after = apart[c + 1]
-            width = wid[rows(c)]
-            z_t = dot(bc_ref[rows(c), :STATE], after.astype(bf16))
-            q2 = q2a[rows(c)] + head_sum(wtd[rows(c)].astype(f32) * z_t)
+            width = wid[span]
+            z_t = dot(bc_ref[span, :STATE], after.astype(bf16))
+            q2 = q2a[span] + head_sum(wtd[span].astype(f32) * z_t)
             ends = jnp.sum((after * hst[c + 1]).reshape(16, 8, WIDE), axis=0)
             end_h = jnp.sum(head_sum(ends), axis=0, keepdims=True)
-            d_s = ds1[rows(c)] - q2
             d_a = lax.dot_general(
-                tri[...], d_s, (((0,), (0,)), ((), ())), precision=highest, preferred_element_type=f32
+                tri[...], ds1[span] - q2, (((0,), (0,)), ((), ())), precision=highest, preferred_element_type=f32
             ) + end_h
             d_w = q2 / width - rate * d_a
-            pre = rawt[rows(c)] + bias_t
-            sig = 1.0 / (1.0 + jnp.exp(-pre))
             dec_g = dec_g - jnp.sum(d_a * (rate * width), axis=0, keepdims=True)
-            bias_g = bias_g + jnp.sum(d_w * sig, axis=0, keepdims=True)
-            return dec_g, bias_g
-
-        zero_row = jnp.zeros((1, 128), f32)
-        dec_g, bias_g = lax.fori_loop(0, CHUNKS, back, (zero_row, zero_row))
+            bias_g = bias_g + jnp.sum(d_w * sig[span], axis=0, keepdims=True)
 
         recv_wait(sbr, 6, 7)
         sums_a = summed(sbr, N_DP)
@@ -627,15 +638,10 @@
             grad[p] = value
             square = square + jnp.sum(jnp.sum(value * value, axis=1, keepdims=True), axis=0, keepdims=True)
         t1[...] = jnp.where(lane < 16, dec_g, jnp.where(lane < 32, bias_g, jnp.where(lane == 32, square, 0.0)))
-        pair = remote(t1, t1r, s_send.at[7, 0], s_recv.at[7, 0], partner, seq)
-        pair.start()
-        pair.wait_recv()
-        t2[...] = t1[...] + t1r[...]
-
-        for a, b, c in far_first:
-            remote(t2, t2r.at[own_q], s_send.at[8, 0], s_recv.at[8, 0], dps[a], seqs[b, c]).start()
-        t2r[own_q] = t2[...]
-        recv_wait(t2r, 8, 63)
+        for d, q in everyone:
+            remote(t1, t2r.at[own_b], s_send.at[8, 0], s_recv.at[8, 0], d, q).start()
+        t2r[own_b] = t1[...]
+        recv_wait(t2r, 8, 127)
         sums_b = jnp.sum(t2r[...], axis=0)
 
         def heads_at(first):
@@ -673,8 +679,7 @@
         for h in range(2):
             send_wait(gi.at[h], 5, 15, h)
         send_wait(sbr, 6, 7)
-        pair.wait_send()
-        send_wait(t2r, 8, 63)
+        send_wait(t2r, 8, 127)
         for k in range(N_Y):
             remote(wgp.at[k], pr.at[k], s_ps.at[k], s_pr.at[k], partner, seq).wait_send()
         for n, p in enumerate(PARTS):

time: 97.1 us -> 95.6 us (0.985)
  Pallas kernels: 96.3 us -> 94.7 us
    pallas_call x1, Pallas kernels: 94.8 us -> 93.2 us  [per_device(): pl.pallas_call(kernel, out_shape=shape((16, WIDE), f32), in_specs=[anywhe...]
where the time goes in v5:
time: 95.6 us; the launch traced here: 95.3 us
  Pallas kernels  94.7 us (99%)
    pallas_call x1, Pallas kernels, per_device(): pl.pallas_call(kernel, out_shape=shape((16, WIDE), f32), in_specs=[anywhe...  93.2 us

profile of v5, /device:TPU:1, one launch (start us, length us, event | category | flops | bytes accessed | tf_op | source)
XLA Modules:
  0.0 95.3 jit_solution(2405704259686017176)
XLA Ops:
  0.6 93.2 %shard_map.163.packed = f32[16,1024]{1,0:T(8,128)} custom-call(bf16[384,1024]{1,0:T(8,128)(2,1)} %bitcast.16, bf16[384,1024]{1,0:T(8,128)(2,1)} %bitcast.17, bf16[384,256]{1,0:T(8,128)(2,1)} %bitcast.19, f32[16,384]{1,0:T(8,128)} %bitcast.20, s32[1,384]{1,0:T(1,128)} %refs_4_.1, s32[8]{0:T(128)} %refs_5_.1, bf16[384,1024]{1,0:T(8,128)(2,1)} %bitcast.18, ...), custom_call_target="tpu_custom_call" | custom-call | tf_op jit(solution)/shard_map/pallas_call | solution.py:720
  93.8 1.5 %shard_map.164 = (f32[1,2]{1,0:T(1,128)}, f32[8,1024]{1,0:T(8,128)}, f32[1,16]{1,0:T(1,128)}, f32[1,16]{1,0:T(1,128)}, f32[1,16]{1,0:T(1,128)}, /*index=5*/f32[1,1024]{1,0:T(1,128)}) custom-call(f32[16,1024]{1,0:T(8,128)} %shard_map.163.packed), custom_call_target="tpu_custom_call" | custom-call | tf_op jit(solution)/shard_map/pallas_call | solution.py:733

commit v6 on v5

--- a/solution.py
+++ b/solution.py
@@ -60,7 +60,7 @@
 
 
 INPUTS = (
-    "x_in", "z_in", "bc_in", "raw_in", "ids_ref", "cnt_ref", "tgt_in", "w_ref", "dec_in", "bias_in", "skip_in", "gain_in",
+    "x_in", "z_in", "bc_in", "raw_hbm", "ids_hbm", "cnt_hbm", "tgt_in", "w_hbm", "dec_hbm", "bias_hbm", "skip_hbm", "gain_hbm",
 )
 OUTPUTS = ("packed_out",)
 PARTS = "yxz"
@@ -74,7 +74,9 @@
     states, sixteen = v((CHUNKS + 1, STATE, WIDE), f32), v((2, N_SEQ, 16, HALF // 2), bf16)
     small, small16, small8 = v((16, 128), f32), v((N_SEQ, 16, 128), f32), v((N_DP, 16, 128), f32)
     named = dict(
-        x_ref=wide_b, z_ref=wide_b, bc_ref=v((TOK, 2 * STATE), bf16), tgt_ref=wide_b, s_in=dma((4,)),
+        raw_in=v((HEADS, TOK), f32), ids_ref=v((1, TOK), jnp.int32), cnt_ref=pltpu.SMEM((N_DP,), jnp.int32),
+        dec_in=v((1, HEADS), f32), bias_in=v((1, HEADS), f32), skip_in=v((1, HEADS), f32),
+        x_ref=wide_b, z_ref=wide_b, bc_ref=v((TOK, 2 * STATE), bf16), tgt_ref=wide_b, s_in=dma((12,)),
         act=wide_f, gat=wide_f, dnf=wide_f, gdn=wide_f, invs=rows_f,
         ex=v((128, WIDE), bf16), red=v((WIDE, 128), bf16), tri=v((CHUNK, CHUNK), f32), par=v((3, 8, 128), f32),
         gain=v((1, WIDE), f32), wown=v((8, WIDE), f32), rawt=rows_f, wid=rows_f, dec_s=rows_f, ent=rows_f,
@@ -108,8 +110,8 @@
 
 
 def program(
-    x_in, z_in, bc_in, raw_in, ids_ref, cnt_ref, tgt_in, w_ref, dec_in, bias_in, skip_in, gain_in,
-    packed_out, x_ref, z_ref, bc_ref, tgt_ref, s_in, act, gat, dnf, gdn, invs,
+    x_in, z_in, bc_in, raw_hbm, ids_hbm, cnt_hbm, tgt_in, w_hbm, dec_hbm, bias_hbm, skip_hbm, gain_hbm,
+    packed_out, raw_in, ids_ref, cnt_ref, dec_in, bias_in, skip_in, x_ref, z_ref, bc_ref, tgt_ref, s_in, act, gat, dnf, gdn, invs,
     ex, red, tri, par, gain, wown, rawt, wid, dec_s, ent, chain, fcol, sc,
     xw, wtd, yin, eexp, gstate, hst, apart, normb, ogb, gb, q2a, ds1, accs,
     hs, hr, hp, hi, gs, gr, gp, gi, cs, cr, wfull, wgp, pr, sa, sar, sb2, sbr, t1, t2r,
@@ -131,6 +133,14 @@
             src_ref=src, dst_ref=dst, send_sem=ss, recv_sem=rs, device_id=at(d, s), device_id_type=MESH
         )
 
+    incoming = (
+        (dec_hbm, dec_in), (bias_hbm, bias_in), (skip_hbm, skip_in), (raw_hbm, raw_in), (ids_hbm, ids_ref), (bc_in, bc_ref),
+        (x_in, x_ref), (w_hbm, wown), (gain_hbm, gain), (z_in, z_ref), (tgt_in, tgt_ref), (cnt_hbm, cnt_ref),
+    )
+    loads = [pltpu.make_async_copy(source, target, s_in.at[n]) for n, (source, target) in enumerate(incoming)]
+    for load in loads:
+        load.start()
+
     barrier = pltpu.get_barrier_semaphore()
 
     dps = [((yy + k) % 4) * 2 + core for k in range(4)]
@@ -148,19 +158,12 @@
                 everyone.append((dps[a] + flip * (1 - 2 * core), seqs[b, c]))
     for d, s in everyone:
         pl.semaphore_signal(barrier, 1, device_id=at(d, s), device_id_type=MESH)
-    loads = [
-        pltpu.make_async_copy(source, target, s_in.at[n])
-        for n, (source, target) in enumerate(((bc_in, bc_ref), (x_in, x_ref), (z_in, z_ref), (tgt_in, tgt_ref)))
-    ]
-    for load in loads:
-        load.start()
 
     row = iota((CHUNK, WIDE), 0)
     col = iota((CHUNK, WIDE), 1)
     ex[...] = jnp.where(((row & 15) == (col >> 6)) & (row < 48), 1.0, 0.0).astype(bf16)
     rrow = iota((WIDE, 128), 0)
     rcol = iota((WIDE, 128), 1)
-    red[...] = jnp.where((rrow >> 6) == (rcol & 15), 1.0, 0.0).astype(bf16)
     ti, tj = iota((CHUNK, CHUNK), 0), iota((CHUNK, CHUNK), 1)
     tri[...] = jnp.where(ti >= tj, 1.0, 0.0)
     rep = jnp.where(iota((HEADS, 128), 0) == (iota((HEADS, 128), 1) & 15), 1.0, 0.0)
@@ -170,15 +173,16 @@
     def tiled(ref):
         return jnp.dot(jnp.broadcast_to(ref[...], (8, HEADS)), rep, precision=highest, preferred_element_type=f32)
 
+    for load in loads[:5]:
+        load.wait()
     par[0] = tiled(dec_in)
     par[1] = tiled(bias_in)
     par[2] = tiled(skip_in)
-    gain[...] = gain_in[...]
-    wown[...] = w_ref[...]
     rawt[...] = lax.dot_general(
         raw_in[...], rep, (((0,), (0,)), ((), ())), precision=highest, preferred_element_type=f32
     )
-    loads[0].wait()
+    loads[5].wait()
+    loads[11].wait()
 
     def expand(v):
         return dot(three_parts(v), ex[...])
@@ -209,7 +213,9 @@
         return carry
 
     lax.fori_loop(0, CHUNKS, prepare, 0)
-    loads[1].wait()
+    loads[6].wait()
+    loads[7].wait()
+    loads[8].wait()
 
     def index_in(p, y, x, z):
         return {"y": y * 16 + x * 4 + z, "x": x * 16 + y * 4 + z, "z": z * 16 + x * 4 + y}[p]
@@ -385,7 +391,8 @@
 
         @pl.when(step == 0)
         def _():
-            loads[2].wait()
+            loads[9].wait()
+            red[...] = jnp.where((rrow >> 6) == (rcol & 15), 1.0, 0.0).astype(bf16)
 
             def once(c, carry):
                 z_f = z_ref[rows(c)].astype(f32)
@@ -395,7 +402,7 @@
                 return carry
 
             lax.fori_loop(0, CHUNKS, once, 0)
-            loads[3].wait()
+            loads[10].wait()
 
         skip_e = expand(jnp.broadcast_to(skip_t, (8, 128)))[0:1]
         gain_e = gain[...]
@@ -714,13 +721,12 @@
 
 def per_device(x, z, bc, raw, ids, counts, target, weight, dec, bias, skip, gain):
     vmem = pl.BlockSpec(memory_space=pltpu.VMEM)
-    smem = pl.BlockSpec(memory_space=pltpu.SMEM)
-    anywhere = pl.BlockSpec(memory_space=pl.ANY)
+    in_hbm = pl.BlockSpec(memory_space=pltpu.HBM)
     shape = jax.ShapeDtypeStruct
     packed = pl.pallas_call(
         kernel,
         out_shape=shape((16, WIDE), f32),
-        in_specs=[anywhere] * 3 + [vmem] * 2 + [smem] + [anywhere] + [vmem] * 5,
+        in_specs=[in_hbm] * 12,
         out_specs=vmem,
         scratch_shapes=list(scratch().values()),
         compiler_params=pltpu.CompilerParams(

time: 95.6 us -> 94.7 us (level)
  no operation moved by 1% of the time
where the time goes in v6:
time: 94.7 us; the launch traced here: 94.5 us
  Pallas kernels  93.9 us (99%)
    pallas_call x1, Pallas kernels, per_device(): pl.pallas_call(kernel, out_shape=shape((16, WIDE), f32), in_specs=[in_hbm...  92.4 us

profile of v6, /device:TPU:1, one launch (start us, length us, event | category | flops | bytes accessed | tf_op | source)
XLA Modules:
  0.0 94.5 jit_solution(2549336812095505326)
XLA Ops:
  0.6 92.4 %shard_map.163.packed = f32[16,1024]{1,0:T(8,128)} custom-call(bf16[384,1024]{1,0:T(8,128)(2,1)} %bitcast.16, bf16[384,1024]{1,0:T(8,128)(2,1)} %bitcast.17, bf16[384,256]{1,0:T(8,128)(2,1)} %bitcast.19, f32[16,384]{1,0:T(8,128)} %bitcast.20, s32[1,384]{1,0:T(1,128)} %refs_4_.1, s32[8]{0:T(128)} %refs_5_.1, bf16[384,1024]{1,0:T(8,128)(2,1)} %bitcast.18, ...), custom_call_target="tpu_custom_call" | custom-call | tf_op jit(solution)/shard_map/pallas_call | solution.py:726
  93.0 1.5 %shard_map.164 = (f32[1,2]{1,0:T(1,128)}, f32[8,1024]{1,0:T(8,128)}, f32[1,16]{1,0:T(1,128)}, f32[1,16]{1,0:T(1,128)}, f32[1,16]{1,0:T(1,128)}, /*index=5*/f32[1,1024]{1,0:T(1,128)}) custom-call(f32[16,1024]{1,0:T(8,128)} %shard_map.163.packed), custom_call_target="tpu_custom_call" | custom-call | tf_op jit(solution)/shard_map/pallas_call | solution.py:739

commit v7 on v6

--- a/solution.py
+++ b/solution.py
@@ -467,7 +467,7 @@
             invs[span] = jnp.broadcast_to(inv, (CHUNK, 128))
             normb[span] = (gated * gain_e * inv).astype(bf16)
             hst[c + 1] = chain[c : c + 1] * state + gstate[c]
-        block = 512
+        block = 1024
         position = seq * TOK + iota((TOK, block), 0)
         scored = jnp.where(position < own_count, 1.0, 0.0)
         losses_8 = jnp.zeros((8, block), f32)
@@ -511,20 +511,6 @@
             for k, piece in zip(pair, pieces):
                 wgp[k] = piece.astype(bf16)
                 remote(wgp.at[k], pr.at[k], s_ps.at[k], s_pr.at[k], partner, seq).start()
-        def small_sums(c, carry):
-            x_f, inv = x_ref[rows(c)].astype(f32), invs[rows(c), 0:1]
-            accs[0] += jnp.sum((dnf[rows(c)] * gat[rows(c)] * inv).reshape(16, 8, WIDE), axis=0)
-            accs[1] += jnp.sum((gb[rows(c)].astype(f32) * x_f).reshape(16, 8, WIDE), axis=0)
-            return carry
-
-        lax.fori_loop(0, CHUNKS, small_sums, 0)
-        gain_g = jnp.sum(accs[0], axis=0, keepdims=True)
-        for r in range(8):
-            sa[r : r + 1, :] = gain_g[:, 128 * r : 128 * (r + 1)]
-        skip_g = head_sum(jnp.broadcast_to(jnp.sum(accs[1], axis=0, keepdims=True), (8, WIDE)))
-        sub = iota((8, 128), 0)
-        sa[8:16, :] = jnp.where(sub == 0, skip_g, jnp.where(sub == 1, jnp.broadcast_to(loss, (8, 128)), 0.0))
-        spread_start(sa, sar, 4)
         for pair in ((1, 2), (3, 0)):
             pieces = grad_rows(*[group(k, core) for k in pair])
             for k, mine in zip(pair, pieces):
@@ -549,6 +535,21 @@
                 slab = part["sb" + p].at[pl.ds(c * 16, 16)]
                 remote(slab, part["ra" + p].at[k - 1], r1s.at[n], r1r.at[n], d, s).start()
 
+        def small_sums(c, carry):
+            x_f, inv = x_ref[rows(c)].astype(f32), invs[rows(c), 0:1]
+            accs[0] += jnp.sum((dnf[rows(c)] * gat[rows(c)] * inv).reshape(16, 8, WIDE), axis=0)
+            accs[1] += jnp.sum((gb[rows(c)].astype(f32) * x_f).reshape(16, 8, WIDE), axis=0)
+            return carry
+
+        lax.fori_loop(0, CHUNKS, small_sums, 0)
+        gain_g = jnp.sum(accs[0], axis=0, keepdims=True)
+        for r in range(8):
+            sa[r : r + 1, :] = gain_g[:, 128 * r : 128 * (r + 1)]
+        skip_g = head_sum(jnp.broadcast_to(jnp.sum(accs[1], axis=0, keepdims=True), (8, WIDE)))
+        sub = iota((8, 128), 0)
+        sa[8:16, :] = jnp.where(sub == 0, skip_g, jnp.where(sub == 1, jnp.broadcast_to(loss, (8, 128)), 0.0))
+        spread_start(sa, sar, 4)
+
         def scatter_plane():
             for p in "xzy":
                 n = PARTS.index(p)
@@ -651,11 +652,9 @@
         recv_wait(t2r, 8, 127)
         sums_b = jnp.sum(t2r[...], axis=0)
 
-        def heads_at(first):
-            picked = jnp.where((lane >= first) & (lane < first + 16), sums_b, 0.0)
-            return jnp.dot(jnp.broadcast_to(picked, (8, 128)), spread, precision=highest, preferred_element_type=f32)[0:1]
-
-        dec_g, bias_g = heads_at(0), heads_at(16)
+        picked = jnp.where(sub8 == (lane8 >> 4), jnp.broadcast_to(sums_b, (8, 128)), 0.0)
+        heads = jnp.dot(picked, spread, precision=highest, preferred_element_type=f32)
+        dec_g, bias_g = heads[0:1], heads[1:2]
         squares = jnp.sum(jnp.where(lane == 32, sums_b, 0.0), axis=1, keepdims=True)
         gain_rows, skip_g, loss_all = sums_a[0:8], sums_a[8:9], sums_a[9:10]
         small = jnp.sum(

time: 94.7 us -> 94.3 us (level)
  no operation moved by 1% of the time
where the time goes in v7:
time: 94.3 us; the launch traced here: 94.2 us
  Pallas kernels  93.5 us (99%)
    pallas_call x1, Pallas kernels, per_device(): pl.pallas_call(kernel, out_shape=shape((16, WIDE), f32), in_specs=[in_hbm...  92.1 us

profile of v7, /device:TPU:1, one launch (start us, length us, event | category | flops | bytes accessed | tf_op | source)
XLA Modules:
  0.0 94.2 jit_solution(8248318859550140035)
XLA Ops:
  0.6 92.1 %shard_map.163.packed = f32[16,1024]{1,0:T(8,128)} custom-call(bf16[384,1024]{1,0:T(8,128)(2,1)} %bitcast.16, bf16[384,1024]{1,0:T(8,128)(2,1)} %bitcast.17, bf16[384,256]{1,0:T(8,128)(2,1)} %bitcast.19, f32[16,384]{1,0:T(8,128)} %bitcast.20, s32[1,384]{1,0:T(1,128)} %refs_4_.1, s32[8]{0:T(128)} %refs_5_.1, bf16[384,1024]{1,0:T(8,128)(2,1)} %bitcast.18, ...), custom_call_target="tpu_custom_call" | custom-call | tf_op jit(solution)/shard_map/pallas_call | solution.py:725
  92.7 1.5 %shard_map.164 = (f32[1,2]{1,0:T(1,128)}, f32[8,1024]{1,0:T(8,128)}, f32[1,16]{1,0:T(1,128)}, f32[1,16]{1,0:T(1,128)}, f32[1,16]{1,0:T(1,128)}, /*index=5*/f32[1,1024]{1,0:T(1,128)}) custom-call(f32[16,1024]{1,0:T(8,128)} %shard_map.163.packed), custom_call_target="tpu_custom_call" | custom-call | tf_op jit(solution)/shard_map/pallas_call | solution.py:738

commit v8 on v7

--- a/solution.py
+++ b/solution.py
@@ -454,7 +454,6 @@
         from_blocks(hi, put_state)
 
         scale = 2.0 / (WIDE * total_f)
-        accs[...] = jnp.zeros(accs.shape, f32)
 
         for c in range(CHUNKS):
             span = slice(c * CHUNK, (c + 1) * CHUNK)
@@ -467,7 +466,7 @@
             invs[span] = jnp.broadcast_to(inv, (CHUNK, 128))
             normb[span] = (gated * gain_e * inv).astype(bf16)
             hst[c + 1] = chain[c : c + 1] * state + gstate[c]
-        block = 1024
+        block = 512
         position = seq * TOK + iota((TOK, block), 0)
         scored = jnp.where(position < own_count, 1.0, 0.0)
         losses_8 = jnp.zeros((8, block), f32)
@@ -534,6 +533,8 @@
                 d, s, c = line_peer(p, k)
                 slab = part["sb" + p].at[pl.ds(c * 16, 16)]
                 remote(slab, part["ra" + p].at[k - 1], r1s.at[n], r1r.at[n], d, s).start()
+
+        accs[...] = jnp.zeros(accs.shape, f32)
 
         def small_sums(c, carry):
             x_f, inv = x_ref[rows(c)].astype(f32), invs[rows(c), 0:1]

time: 94.3 us -> 94.3 us (level)
  no operation moved by 1% of the time
where the time goes in v8:
time: 94.3 us; the launch traced here: 94.2 us
  Pallas kernels  93.5 us (99%)
    pallas_call x1, Pallas kernels, per_device(): pl.pallas_call(kernel, out_shape=shape((16, WIDE), f32), in_specs=[in_hbm...  92 us

profile of v8, /device:TPU:1, one launch (start us, length us, event | category | flops | bytes accessed | tf_op | source)
XLA Modules:
  0.0 94.2 jit_solution(6316111040073741810)
XLA Ops:
  0.6 92.0 %shard_map.163.packed = f32[16,1024]{1,0:T(8,128)} custom-call(bf16[384,1024]{1,0:T(8,128)(2,1)} %bitcast.16, bf16[384,1024]{1,0:T(8,128)(2,1)} %bitcast.17, bf16[384,256]{1,0:T(8,128)(2,1)} %bitcast.19, f32[16,384]{1,0:T(8,128)} %bitcast.20, s32[1,384]{1,0:T(1,128)} %refs_4_.1, s32[8]{0:T(128)} %refs_5_.1, bf16[384,1024]{1,0:T(8,128)(2,1)} %bitcast.18, ...), custom_call_target="tpu_custom_call" | custom-call | tf_op jit(solution)/shard_map/pallas_call | solution.py:726
  92.7 1.5 %shard_map.164 = (f32[1,2]{1,0:T(1,128)}, f32[8,1024]{1,0:T(8,128)}, f32[1,16]{1,0:T(1,128)}, f32[1,16]{1,0:T(1,128)}, f32[1,16]{1,0:T(1,128)}, /*index=5*/f32[1,1024]{1,0:T(1,128)}) custom-call(f32[16,1024]{1,0:T(8,128)} %shard_map.163.packed), custom_call_target="tpu_custom_call" | custom-call | tf_op jit(solution)/shard_map/pallas_call | solution.py:739
